TPU v7x, 32 devices: a whole 2x2x4 slice. The times are simulated.
32 devices in a mesh: dp: 8 (over y, x, core), tensor: 4 (over z).
Axes of the slice: x: 2, y: 2, z: 4, core: 2. Of those that a mesh axis runs over, the one named last changes fastest.
Arguments:
- gradient: float32 [5120, 27648], P('dp', 'tensor'), may hold values from -6 to 6
- momentum: float32 [5120, 27648], P('dp', 'tensor'), may hold values from -6 to 6
- right_factor: float32 [27648, 256], P('tensor'), may hold values from -6 to 6
Outputs:
- update: float32 [5120, 27648], P('dp', 'tensor')
- new_momentum: float32 [5120, 27648], P('dp', 'tensor')
- new_right: float32 [27648, 256], P('tensor')
All inputs are finite; a program needn't handle non-finite values.
Results may differ from a plain program's by a relative error of at most 0.000098.
Values sent between devices are 32-bit elements; how exact they have to be, the bound alone decides.
No kernel may reach another device: no remote copies, remote signals or barrier semaphores. Data moves between devices by JAX's collectives and lax.ppermute only.
A program may use at most 192 MiB of HBM per device.

v0:
```python
import functools

import jax
import jax.numpy as jnp
from jax import lax
from jax.experimental import pallas as pl
from jax.experimental.pallas import tpu as pltpu
from jax.sharding import PartitionSpec as P


F32 = jnp.float32
BF16 = jnp.bfloat16
HIGH = lax.Precision.HIGHEST
LANES = 128

NN = (((1,), (0,)), ((), ()))
NT = (((1,), (1,)), ((), ()))
TN = (((0,), (0,)), ((), ()))


HBM = pl.BlockSpec(memory_space=pltpu.HBM)
VMEM = pl.BlockSpec(memory_space=pltpu.VMEM)
SMEM = pl.BlockSpec(memory_space=pltpu.SMEM)


def params(mib):
    return pltpu.CompilerParams(vmem_limit_bytes=mib * 1024 * 1024)


def cost(flops, moved):
    return pl.CostEstimate(flops=int(flops), bytes_accessed=int(moved), transcendentals=0)


def split(x):
    hi = x.astype(BF16)
    lo = (x - hi.astype(F32)).astype(BF16)
    return hi, lo


def dot(a, b, dims):
    return lax.dot_general(a, b, dims, preferred_element_type=F32)


def dot3(ah, al, bh, bl, dims):
    return dot(ah, bh, dims) + (dot(ah, bl, dims) + dot(al, bh, dims))


def dot_high(a, b, dims):
    return lax.dot_general(a, b, dims, precision=HIGH, preferred_element_type=F32)


def column_block(cols):
    blocks = cols // LANES
    return LANES * max(k for k in range(1, 9) if blocks % k == 0)


DEPTH = 4


def left_kernel(first, which, part, at, g, m, *refs):
    if first:
        r, buffer, rh, rl, *outs, gs, ms, rs, sems = refs
    else:
        rh, rl, buffer, *outs, gs, ms, sems = refs
    depth, n, wide = gs.shape
    steps = g.shape[1] // wide
    top = at[which] * (g.shape[0] // 2) + part * n
    rows = pl.ds(pl.multiple_of(top, GROUP), n)

    def copies(j, slot):
        part = pl.ds(pl.multiple_of(j * wide, LANES), wide)
        some = [
            pltpu.make_async_copy(g.at[rows, part], gs.at[slot], sems.at[0, slot]),
            pltpu.make_async_copy(m.at[rows, part], ms.at[slot], sems.at[1, slot]),
        ]
        if first:
            some.append(pltpu.make_async_copy(r.at[part, :], rs.at[slot], sems.at[2, slot]))
        return some

    for j in range(min(depth, steps)):
        for copy in copies(j, j):
            copy.start()
    for out in outs:
        out[...] = jnp.zeros_like(out)

    def body(j, _):
        slot = lax.rem(j, depth)
        part = pl.ds(pl.multiple_of(j * wide, LANES), wide)
        for copy in copies(j, slot):
            copy.wait()
        b = gs[slot] + ms[slot]
        buffer[:, part] = b
        bh, bl = split(b)
        if first:
            rh[part, :], rl[part, :] = split(rs[slot])
        term = dot3(bh, bl, rh[part, :], rl[part, :], NN)
        size = n // len(outs)
        for i, out in enumerate(outs):
            out[...] += term[i * size : (i + 1) * size]

        @pl.when(j + depth < steps)
        def _():
            for copy in copies(j + depth, slot):
                copy.start()

        return 0

    lax.fori_loop(0, steps, body, 0)


def left_rows(at, which, part, parts, gradient, momentum, right, padded):
    first = not isinstance(right, tuple)
    right = (right,) if first else right
    rows, cols = gradient.shape
    rank = right[0].shape[1]
    wide = column_block(cols)
    n = rows // 2 if first else rows // (2 * parts)
    outs = parts if first else 1
    terms = [pltpu.VMEM((cols, rank), BF16)] * 2 if first else []
    return pl.pallas_call(
        functools.partial(left_kernel, first, which, part),
        in_specs=[SMEM, HBM, HBM] + ([HBM] if first else [VMEM, VMEM]),
        out_specs=[VMEM] * (1 + len(terms) + outs),
        out_shape=[pltpu.VMEM((n, padded), F32)]
        + terms
        + [jax.ShapeDtypeStruct((rows // (2 * parts), rank), F32)] * outs,
        scratch_shapes=[pltpu.VMEM((DEPTH, n, wide), F32)] * 2
        + ([pltpu.VMEM((DEPTH, wide, rank), F32)] if first else [])
        + [pltpu.SemaphoreType.DMA((3 if first else 2, DEPTH))],
        compiler_params=params(34 if first else 30),
        cost_estimate=cost(6 * n * cols * rank, 4 * (2 * n * cols + cols * rank)),
        name="left_rows",
    )(at, gradient, momentum, *right)


def total_kernel(count, *refs):
    ins, outs = refs[:count], refs[count:]
    n = outs[0].shape[0]
    for i, out in enumerate(outs):
        terms = [x[i * n : (i + 1) * n, :] for x in ins]
        while len(terms) > 1:
            terms = [terms[k] + terms[k + 1] for k in range(0, len(terms), 2)]
        out[...] = terms[0]


def total(*blocks, parts=1):
    rows, rank = blocks[0].shape
    outs = pl.pallas_call(
        functools.partial(total_kernel, len(blocks)),
        in_specs=[VMEM] * len(blocks),
        out_specs=[VMEM] * parts,
        out_shape=[jax.ShapeDtypeStruct((rows // parts, rank), F32)] * parts,
        compiler_params=params(6),
        cost_estimate=cost(rows * rank, 4 * (len(blocks) + 1) * rows * rank),
        name="total",
    )(*blocks)
    return outs[0] if parts == 1 else outs


def gram_kernel(place, at, *refs):
    pieces, (left, lh, ll, send, keep, gram) = refs[:-6], refs[-6:]
    n = pieces[0].shape[0]
    for i, piece in enumerate(pieces):
        x = piece[...]
        rows = pl.ds(i * n, n)
        left[rows, :] = x
        lh[rows, :], ll[rows, :] = split(x)
    half = left.shape[0] // 2
    own, other = left[:half, :], left[half:, :]
    gram[...] = dot_high(own, own, TN) + dot_high(other, other, TN)
    n, core = send.shape[0], at[place]
    send[...] = gram[pl.ds(pl.multiple_of((1 - core) * n, GROUP), n), :]
    keep[...] = gram[pl.ds(pl.multiple_of(core * n, GROUP), n), :]


def gram_of(at, place, pieces):
    rank = pieces[0].shape[1]
    rows = sum(p.shape[0] for p in pieces)
    return pl.pallas_call(
        functools.partial(gram_kernel, place),
        in_specs=[SMEM] + [VMEM] * len(pieces),
        out_specs=[VMEM] * 5,
        out_shape=[
            jax.ShapeDtypeStruct((rows, rank), F32),
            jax.ShapeDtypeStruct((rows, rank), BF16),
            jax.ShapeDtypeStruct((rows, rank), BF16),
            jax.ShapeDtypeStruct((rank // 2, rank), F32),
            jax.ShapeDtypeStruct((rank // 2, rank), F32),
        ],
        scratch_shapes=[pltpu.VMEM((rank, rank), F32)],
        compiler_params=params(8),
        cost_estimate=cost(12 * rows * rank * rank, 12 * rows * rank),
        name="gram_of",
    )(at, *pieces)


def w_term(unit, width, lh, ll, buffers):
    part = pl.ds(pl.multiple_of(unit * width, LANES), width)
    bh, bl = split(jnp.concatenate([x[:, part] for x in buffers], axis=0))
    return dot3(bh, bl, lh[...], ll[...], TN)


def w_send_kernel(place, at, lh, ll, *refs):
    *buffers, out = refs
    out[...] = w_term(at[place + pl.program_id(0)], out.shape[0], lh, ll, buffers)


def w_keep_kernel(place, at, got, lh, ll, *refs):
    *buffers, send, keep = refs
    i, width = pl.program_id(0), send.shape[0]
    value = w_term(at[place + i], width, lh, ll, buffers) + got[...]

    @pl.when(i == 0)
    def _():
        send[...] = value

    @pl.when(i == 1)
    def _():
        keep[...] = value


def w_cost(rows, rank, unit):
    return cost(2 * 6 * rows * unit * rank, 2 * 4 * unit * rank)


def w_send(at, place, lh, ll, unit, *buffers):
    rows, rank = lh.shape
    return pl.pallas_call(
        functools.partial(w_send_kernel, place),
        grid_spec=pltpu.PrefetchScalarGridSpec(
            num_scalar_prefetch=1,
            grid=(2,),
            in_specs=[VMEM] * (2 + len(buffers)),
            out_specs=pl.BlockSpec((unit, rank), lambda i, at: (i, 0)),
        ),
        out_shape=jax.ShapeDtypeStruct((2 * unit, rank), F32),
        compiler_params=params(12),
        cost_estimate=w_cost(rows, rank, unit),
        name="w_send",
    )(at, lh, ll, *buffers)


def w_keep(at, place, got, lh, ll, unit, *buffers):
    rows, rank = lh.shape
    one = pl.BlockSpec((unit, rank), lambda i, at: (0, 0))
    return pl.pallas_call(
        functools.partial(w_keep_kernel, place),
        grid_spec=pltpu.PrefetchScalarGridSpec(
            num_scalar_prefetch=1,
            grid=(2,),
            in_specs=[pl.BlockSpec((unit, rank), lambda i, at: (at[place + 2 + i], 0))]
            + [VMEM] * (2 + len(buffers)),
            out_specs=[one, one],
        ),
        out_shape=[jax.ShapeDtypeStruct((unit, rank), F32)] * 2,
        compiler_params=params(14),
        cost_estimate=w_cost(rows, rank, unit),
        name="w_keep",
    )(at, got, lh, ll, *buffers)


GROUP = 8


def factor_group(rows, at):
    full = (GROUP, LANES)
    columns = [jnp.broadcast_to(rows[:, at + j : at + j + 1], full) for j in range(GROUP)]
    a = {
        (i, j): jnp.broadcast_to(columns[j][i : i + 1, :], full)
        for j in range(GROUP)
        for i in range(j, GROUP)
    }
    low, c = {}, {}
    for k in range(GROUP):
        c[k, k] = lax.rsqrt(a[k, k])
        for i in range(k + 1, GROUP):
            low[i, k] = a[i, k] * c[k, k]
        for j in range(k + 1, GROUP):
            for i in range(j, GROUP):
                a[i, j] = a[i, j] - low[i, k] * low[j, k]
        for j in range(k):
            total = low[k, j] * c[j, j]
            for i in range(j + 1, k):
                total = total + low[k, i] * c[i, j]
            c[k, j] = -c[k, k] * total
    return c


def spread(x, width):
    return jnp.concatenate([x] * (width // LANES), axis=1)


def eliminate(block):
    size, width = block.shape
    sub = lax.broadcasted_iota(jnp.int32, (GROUP, LANES), 0)
    groups = [block[i : i + GROUP, :] for i in range(0, size, GROUP)]
    for p in range(len(groups)):
        at = p * GROUP
        rows = groups[p]
        c = factor_group(rows, at)
        done = None
        for j in range(GROUP):
            col = jnp.zeros((GROUP, LANES), F32)
            for i in range(j, GROUP):
                col = jnp.where(sub == i, c[i, j], col)
            term = spread(col, width) * jnp.broadcast_to(rows[j : j + 1, :], (GROUP, width))
            done = term if done is None else done + term
        groups[p] = done
        if p + 1 == len(groups):
            break
        solved = None
        for k in range(GROUP):
            col = jnp.zeros((GROUP, LANES), F32)
            for j in range(k + 1):
                col = jnp.where(sub == j, c[k, j], col)
            term = spread(col, width) * jnp.broadcast_to(done[k : k + 1, :], (GROUP, width))
            solved = term if solved is None else solved + term
        for q in range(p + 1, len(groups)):
            x = groups[q]
            total = None
            for j in range(GROUP):
                term = jnp.broadcast_to(x[:, at + j : at + j + 1], (GROUP, width)) * jnp.broadcast_to(
                    solved[j : j + 1, :], (GROUP, width)
                )
                total = term if total is None else total + term
            groups[q] = x - total
    return jnp.concatenate(groups, axis=0)


def chol_kernel(place, at, mine, beside, left, x_out, oh, ol, work):
    n, rank = mine.shape
    size = min(64, rank)
    core = at[place]
    work[pl.ds(pl.multiple_of(core * n, GROUP), n), :rank] = mine[...]
    work[pl.ds(pl.multiple_of((1 - core) * n, GROUP), n), :rank] = beside[...]
    r = lax.broadcasted_iota(jnp.int32, (rank, rank), 0)
    c = lax.broadcasted_iota(jnp.int32, (rank, rank), 1)
    work[:, rank:] = jnp.where(r == c, 1.0, 0.0).astype(F32)

    def step(b, _):
        top = pl.multiple_of(b * size, size)
        rows = pl.ds(top, size)
        width = 2 * rank
        block = pltpu.roll(work[rows, :], lax.rem(width - top, width), 1)
        block = pltpu.roll(eliminate(block), top, 1)
        x_out[rows, :] = block[:, rank:]

        @pl.when(b + 1 < rank // size)
        def _():
            work[...] -= dot_high(block[:, :rank], block, TN)

        return 0

    lax.fori_loop(0, rank // size, step, 0)
    h, l = split(dot_high(left[...], x_out[...], NT))
    oh[...] = h
    ol[...] = l


def chol_inverse(at, place, mine, beside, left):
    rows, rank = left.shape
    return pl.pallas_call(
        functools.partial(chol_kernel, place),
        in_specs=[SMEM] + [VMEM] * 3,
        out_specs=[VMEM] * 3,
        out_shape=[
            jax.ShapeDtypeStruct((rank, rank), F32),
            jax.ShapeDtypeStruct((rows, rank), BF16),
            jax.ShapeDtypeStruct((rows, rank), BF16),
        ],
        scratch_shapes=[pltpu.VMEM((rank, 2 * rank), F32)],
        compiler_params=params(8),
        cost_estimate=cost(4e9, 4 * rows * rank),
        name="chol_inverse",
    )(at, mine, beside, left)


def right_kernel(place, cols, at, ka, ga, kb, gb, x, ra, rb, squares):
    rows, rank = ka.shape
    total = jnp.zeros((1, rank), F32)
    for i, (k, g, out) in enumerate(((ka, ga, ra), (kb, gb, rb))):
        value = dot_high(k[...] + g[...], x[...], NT)
        out[...] = value
        row = lax.broadcasted_iota(jnp.int32, (rows, rank), 0) + at[place + i]
        value = jnp.where(row < cols, value, 0.0)
        total = total + jnp.sum(value * value, axis=0, keepdims=True)
    squares[...] = jnp.broadcast_to(total, squares.shape)


def right_rows(at, place, cols, ka, ga, kb, gb, x):
    rows, rank = ka.shape
    vm = pl.BlockSpec(memory_space=pltpu.VMEM)
    return pl.pallas_call(
        functools.partial(right_kernel, place, cols),
        in_specs=[pl.BlockSpec(memory_space=pltpu.SMEM)] + [vm] * 5,
        out_specs=[vm] * 3,
        out_shape=[jax.ShapeDtypeStruct((rows, rank), F32)] * 2
        + [jax.ShapeDtypeStruct((GROUP, rank), F32)],
        compiler_params=params(8),
        cost_estimate=cost(24 * rows * rank * rank, 24 * rows * rank),
        name="right_rows",
    )(at, ka, ga, kb, gb, x)


def join_kernel(place, at, x, y, both, *parts):
    n, t = x.shape[0], at[place]
    both[pl.ds(pl.multiple_of(t * n, GROUP), n), :] = x[...]
    both[pl.ds(pl.multiple_of((1 - t) * n, GROUP), n), :] = y[...]
    top = 0
    for out in parts:
        out[...] = both[top : top + out.shape[0], :]
        top += out.shape[0]


def join(at, place, x, y, sizes):
    rows, rank = x.shape
    return pl.pallas_call(
        functools.partial(join_kernel, place),
        in_specs=[SMEM, VMEM, VMEM],
        out_specs=[VMEM] * (1 + len(sizes)),
        out_shape=[jax.ShapeDtypeStruct((n, rank), F32) for n in [2 * rows, *sizes]],
        compiler_params=params(6),
        cost_estimate=cost(rows * rank, 16 * rows * rank),
        name="join",
    )(at, x, y)


def halve_kernel(place, at, x, y, send, keep):
    n, t = send.shape[0], at[place]
    for part, out in ((1 - t, send), (t, keep)):
        rows = pl.ds(pl.multiple_of(part * n, GROUP), n)
        out[...] = x[rows, :] + y[rows, :]


def halve(at, place, x, y):
    rows, rank = x.shape
    return pl.pallas_call(
        functools.partial(halve_kernel, place),
        in_specs=[SMEM, VMEM, VMEM],
        out_specs=[VMEM, VMEM],
        out_shape=[jax.ShapeDtypeStruct((rows // 2, rank), F32)] * 2,
        compiler_params=params(6),
        cost_estimate=cost(rows * rank, 12 * rows * rank),
        name="halve",
    )(at, x, y)


SLOTS = 2


def final_kernel(held, place, group, unit, total_cols, factor, at, *refs):
    pieces, (squares, oh, ol), buffers = refs[:4], refs[4:7], refs[7 : 7 + held]
    update, momentum, new_right, stage_m, stage_u, stage_r, lh, ll, high, low, sems = refs[-11:]
    start, count = group
    n, rows = count * LANES, oh.shape[0]
    half = rows // 2
    blocks = update.shape[1] // LANES
    *own, other = buffers
    ranges = [(x, 0, i * x.shape[0]) for i, x in enumerate(own)] + [(other, 1, 0)]
    scale = jnp.sqrt(squares[0:1, :] / total_cols + 1e-06)
    lh[:rows, :] = oh[...]
    ll[:rows, :] = ol[...]
    lh[rows:, :], ll[rows:, :] = split((oh[...].astype(F32) + ol[...].astype(F32)) * (factor / scale))

    def each_copy(k, act):
        slot = lax.rem(k, SLOTS)
        first = at[place + k] * (unit // LANES) + start
        for j in range(count):

            @pl.when(first + j < blocks)
            def _(j=j):
                here = pl.ds(j * LANES, LANES)
                there = pl.ds(pl.multiple_of((first + j) * LANES, LANES), LANES)
                for i, (a, b) in enumerate(
                    (
                        (stage_m.at[slot, :, here], momentum.at[:, there]),
                        (stage_u.at[slot, :, here], update.at[:, there]),
                        (stage_r.at[slot, here, :], new_right.at[there, :]),
                    )
                ):
                    act(pltpu.make_async_copy(a, b, sems.at[i, slot, j]))

    def body(k, _):
        slot = lax.rem(k, SLOTS)

        @pl.when(k >= SLOTS)
        def _():
            each_copy(k - SLOTS, lambda copy: copy.wait())

        for i, piece in enumerate(pieces):

            @pl.when(k == i)
            def _(piece=piece):
                right = piece[...]
                high[...], low[...] = split(right)
                stage_r[slot] = right / scale

        part = pl.ds(pl.multiple_of(at[place + k] * unit + start * LANES, LANES), n)
        value = dot(lh[...], high[...], NT) + dot(ll[...], high[...], NT)
        rest = dot(lh[rows:, :], low[...], NT)
        for buffer, h, past in ranges:
            size, top = buffer.shape[0], h * half + past
            here = pl.ds(pl.multiple_of(at[h] * half + past, GROUP), size)
            stage_m[slot, here, :] = buffer[:, part] - 0.05 * value[top : top + size]
            stage_u[slot, here, :] = value[rows + top : rows + top + size] + rest[top : top + size]
        each_copy(k, lambda copy: copy.start())
        return 0

    lax.fori_loop(0, 4, body, 0)
    for k in range(4 - SLOTS, 4):
        each_copy(k, lambda copy: copy.wait())


def final(at, place, group, unit, pieces, squares, oh, ol, buffers, sizes, before):
    rows, rank = oh.shape
    cols, total_rows, total_cols = sizes
    factor = (total_rows / rank) ** 0.5
    n = group[1] * LANES
    return pl.pallas_call(
        functools.partial(final_kernel, len(buffers), place, group, unit, total_cols, factor),
        in_specs=[SMEM] + [VMEM] * (7 + len(buffers)) + [HBM] * len(before),
        out_specs=[HBM] * 3,
        out_shape=[
            jax.ShapeDtypeStruct((rows, cols), F32),
            jax.ShapeDtypeStruct((rows, cols), F32),
            jax.ShapeDtypeStruct((cols, rank), F32),
        ],
        scratch_shapes=[
            pltpu.VMEM((SLOTS, rows, n), F32),
            pltpu.VMEM((SLOTS, rows, n), F32),
            pltpu.VMEM((SLOTS, n, rank), F32),
            pltpu.VMEM((2 * rows, rank), BF16),
            pltpu.VMEM((2 * rows, rank), BF16),
            pltpu.VMEM((n, rank), BF16),
            pltpu.VMEM((n, rank), BF16),
            pltpu.SemaphoreType.DMA((3, SLOTS, group[1])),
        ],
        input_output_aliases={len(buffers) + 8 + i: i for i in range(len(before))},
        compiler_params=params(28),
        cost_estimate=cost(48 * rows * n * rank, 32 * rows * n),
        name="final",
    )(at, *pieces, squares, oh, ol, *buffers, *before)


def power_of_two(n):
    return n & (n - 1) == 0


def bits_of(n):
    return list(range(n.bit_length() - 1))


def swap(x, axis, *places):
    n = lax.axis_size(axis)
    mask = sum(1 << bit for bit in places)
    return lax.ppermute(x, axis, [(i, i ^ mask) for i in range(n)])


def spread_sum(x, bits):
    for b in bits[3:]:
        x = total(x, swap(x, "dp", b))
    b, c = bits[1:3]
    others = [swap(x, "dp", *m) for m in ((b,), (c,), (b, c))]
    return total(x, *others)


def on_device(gradient, momentum, right_factor):
    rows, cols = gradient.shape
    n_dp, n_tp = lax.axis_size("dp"), lax.axis_size("tensor")
    d, z = lax.axis_index("dp"), lax.axis_index("tensor")
    bits = bits_of(n_dp)

    unit = LANES * (-(-cols // (8 * LANES)))
    orders = [bits[1:], bits[1:][::-1]]
    table = []

    def put(*values):
        table.extend(values)
        return len(table) - len(values)

    bit_of = lambda b: (d >> b) & 1
    s, core = z & 1, d & 1
    put(s, 1 - s)
    core_at = put(core)
    send_at, keep_at, bit_at, near, far, first = [], [], [], [], [], []
    for h, order in enumerate(orders):
        t = bit_of(order[0])
        base, beside = 4 * h + 2 * core, 4 * h + 2 * (1 - core)
        send_at.append(put(beside, beside + 1))
        keep_at.append(put(base + 1 - t, base + t, 1 - t, t))
        bit_at.append({b: put(bit_of(b)) for b in order[1:]})
        near += [base + t, beside + t]
        far += [base + 1 - t, beside + 1 - t]
        at, n = (base + t) * unit, unit
        for b in order[1:]:
            n = n // 2
            at = at + bit_of(b) * n
        first.append(at)
    near_at, far_at, first_at = put(*near), put(*far), put(*first)
    at = jnp.stack([jnp.asarray(v, jnp.int32) for v in table])

    parts = 2 if rows % (4 * GROUP) == 0 else 1
    other, rh, rl, *away = left_rows(at, 1, 0, parts, gradient, momentum, right_factor, 8 * unit)
    own, mine = [], []
    for i in range(parts):
        x, y = left_rows(at, 0, i, parts, gradient, momentum, (rh, rl), 8 * unit)
        own.append(x)
        mine.append(y)
    held = (*own, other)
    if power_of_two(n_tp) and n_tp > 1:
        pieces = []
        for i in range(parts):
            got = swap(away[i], "tensor", 0)
            pieces.append(total(mine[i], got))
        for bit in bits_of(n_tp)[1:]:
            for i in range(parts):
                got = swap(pieces[i], "tensor", bit)
                pieces[i] = total(pieces[i], got)
        for i in range(parts):
            pieces.append(swap(pieces[i], "tensor", 0))
    else:
        mine, away = jnp.concatenate(mine), jnp.concatenate(away)
        both = lax.psum(jnp.where(s == 0, jnp.stack([mine, away]), jnp.stack([away, mine])), "tensor")
        pieces = [lax.dynamic_index_in_dim(both, i, 0, False) for i in (s, 1 - s)]

    left, lh, ll, send, gram = gram_of(at, core_at, pieces)
    got = swap(send, "dp", 0)
    gram = spread_sum(total(gram, got), bits)
    gram_beside = swap(gram, "dp", 0)

    got = []
    for h in range(2):
        sent = w_send(at, send_at[h], lh, ll, unit, *held)
        got.append(swap(sent, "dp", 0))
    kept = []
    for h, order in enumerate(orders):
        send, keep = w_keep(at, keep_at[h], got[h], lh, ll, unit, *held)
        recv = swap(send, "dp", order[0])
        for b in order[1:]:
            send, keep = halve(at, bit_at[h][b], keep, recv)
            recv = swap(send, "dp", b)
        kept += [keep, recv]

    x_inv, oh, ol = chol_inverse(at, core_at, gram, gram_beside, left)
    *right, squares = right_rows(at, first_at, cols, *kept, x_inv)
    if power_of_two(n_tp):
        for b in bits_of(n_tp):
            squares = total(squares, swap(squares, "tensor", b))
    else:
        squares = lax.psum(squares, "tensor")
    got = swap(squares, "dp", 0)
    squares = total(squares, got)
    squares = spread_sum(squares, bits)

    blocks = unit // LANES
    groups = ((0, blocks - blocks // 2), (blocks - blocks // 2, blocks // 2))
    near, far = [], ([], [])
    for h, (order, x) in enumerate(zip(orders, right)):
        parts = [x]
        for b in order[:0:-1]:
            y = swap(x, "dp", b)
            last = 2 * x.shape[0] == unit
            x, *parts = join(
                at, bit_at[h][b], x, y, [count * LANES for _, count in groups] if last else []
            )
        for g, part in enumerate(parts):
            y = swap(part, "dp", order[0])
            far[g].extend([y, swap(y, "dp", 0)])
        near.extend([x, swap(x, "dp", 0)])

    same = (squares, oh, ol, held, (cols, rows * n_dp, cols * n_tp))
    outs = final(at, near_at, (0, blocks), unit, near, *same, ())
    for g in range(2):
        outs = final(at, far_at, groups[g], unit, far[g], *same, outs)
    return tuple(outs)


def solution(mesh):
    return jax.shard_map(
        on_device,
        mesh=mesh,
        in_specs=(P("dp", "tensor"), P("dp", "tensor"), P("tensor", None)),
        out_specs=(P("dp", "tensor"), P("dp", "tensor"), P("tensor", None)),
        check_vma=False,
    )
```

profile of v0, /device:TPU:0, one launch (start us, length us, event | category | flops | bytes accessed | tf_op | source)
XLA Modules:
  0.0 193.3 jit_solution(11087964676429868542)
XLA Ops:
  0.7 0.1 stack.93.at
  0.8 9.6 %left_rows.3 = (f32[320,7168]{1,0:T(8,128)S(1)}, bf16[6912,256]{1,0:T(8,128)(2,1)S(1)}, bf16[6912,256]{1,0:T(8,128)(2,1)S(1)}, f32[160,256]{1,0:T(8,128)S(1)}, f32[160,256]{1,0:T(8,128)S(1)}) custom-call(s32[27]{0:T(128)S(1)} %stack.93.at, f32[640,6912]{1,0:T(8,128)} %g.5, f32[640,6912]{1,0:T(8,128)} %m.5, f32[6912,256]{1,0:T(8,128)} %refs_0_.1), custom_call_target="tpu_custom_call" | custom-call | flops 3397386240 | bytes 24772608 | tf_op jit(solution)/shard_map/left_rows/pallas_call | solution.py:120
  10.4 3.1 %collective-permute-start.2 = (f32[160,256]{1,0:T(8,128)S(1)}, f32[160,256]{1,0:T(8,128)S(1)}, u32[]{:S(2)}, u32[]{:S(2)}) collective-permute-start(f32[160,256]{1,0:T(8,128)S(1)} %get-tuple-element.48), channel_id=1, source_target_pairs={{0,1},{1,0},{2,3},{3,2},{4,5},{5,4},{6,7},{7,6},{8,9},{9,8},{10,11... | collective-permute-start | bytes 491528 | tf_op jit(solution)/shard_map/ppermute | solution.py:556
  13.5 0.1 collective-permute-start
  13.6 5.3 %left_rows.5 = (f32[160,7168]{1,0:T(8,128)S(1)}, f32[160,256]{1,0:T(8,128)S(1)}) custom-call(s32[27]{0:T(128)S(1)} %stack.93.at, f32[640,6912]{1,0:T(8,128)} %g.5, f32[640,6912]{1,0:T(8,128)} %m.5, bf16[6912,256]{1,0:T(8,128)(2,1)S(1)} %get-tuple-element.43.refs_0_, bf16[6912,256]{1,0:T(8,128)(2,1)S(1)} %get-tuple-element.44.refs_1_), custom_call_target="tpu_custom_call" | custom-call | flops 1698693120 | bytes 15925248 | tf_op jit(solution)/shard_map/left_rows/pallas_call | solution.py:120
  18.9 5.2 %left_rows.4 = (f32[160,7168]{1,0:T(8,128)S(1)}, f32[160,256]{1,0:T(8,128)S(1)}) custom-call(s32[27]{0:T(128)S(1)} %stack.93.at, f32[640,6912]{1,0:T(8,128)} %g.5, f32[640,6912]{1,0:T(8,128)} %m.5, bf16[6912,256]{1,0:T(8,128)(2,1)S(1)} %get-tuple-element.43.refs_0_, bf16[6912,256]{1,0:T(8,128)(2,1)S(1)} %get-tuple-element.44.refs_1_), custom_call_target="tpu_custom_call" | custom-call | flops 1698693120 | bytes 15925248 | tf_op jit(solution)/shard_map/left_rows/pallas_call | solution.py:120
  24.2 3.0 %collective-permute-start.3 = (f32[160,256]{1,0:T(8,128)S(1)}, f32[160,256]{1,0:T(8,128)S(1)}, u32[]{:S(2)}, u32[]{:S(2)}) collective-permute-start(f32[160,256]{1,0:T(8,128)S(1)} %total.12.refs_0_), channel_id=1, source_target_pairs={{0,2},{1,3},{2,0},{3,1},{4,6},{5,7},{6,4},{7,5},{8,10},{9,11},{10,... | collective-permute-start | bytes 491528 | tf_op jit(solution)/shard_map/ppermute | solution.py:556
  27.2 0.1 collective-permute-start.1
  27.3 11.7 %collective-permute-done.3.refs_1_ = f32[160,256]{1,0:T(8,128)S(1)} collective-permute-done((f32[160,256]{1,0:T(8,128)S(1)}, f32[160,256]{1,0:T(8,128)S(1)}, u32[]{:S(2)}, u32[]{:S(2)}) %collective-permute-start.3) | collective-permute-done | bytes 163872 | tf_op jit(solution)/shard_map/ppermute | solution.py:556
  39.0 0.1 collective-permute-start.5
  39.1 2.4 %collective-permute-done.1.refs_1_ = f32[160,256]{1,0:T(8,128)S(1)} collective-permute-done((f32[160,256]{1,0:T(8,128)S(1)}, f32[160,256]{1,0:T(8,128)S(1)}, u32[]{:S(2)}, u32[]{:S(2)}) %collective-permute-start.1) | collective-permute-done | bytes 163872 | tf_op jit(solution)/shard_map/ppermute | solution.py:556
  41.5 0.7 collective-permute-start.4
  42.2 4.0 %collective-permute-done.5.refs_3_ = f32[160,256]{1,0:T(8,128)S(1)} collective-permute-done((f32[160,256]{1,0:T(8,128)S(1)}, f32[160,256]{1,0:T(8,128)S(1)}, u32[]{:S(2)}, u32[]{:S(2)}) %collective-permute-start.5) | collective-permute-done | bytes 163872 | tf_op jit(solution)/shard_map/ppermute | solution.py:556
  46.2 2.2 %collective-permute-done.4.refs_2_ = f32[160,256]{1,0:T(8,128)S(1)} collective-permute-done((f32[160,256]{1,0:T(8,128)S(1)}, f32[160,256]{1,0:T(8,128)S(1)}, u32[]{:S(2)}, u32[]{:S(2)}) %collective-permute-start.4) | collective-permute-done | bytes 163872 | tf_op jit(solution)/shard_map/ppermute | solution.py:556
  48.4 1.7 gram_of.1
  50.1 3.2 %w_send.3 = f32[1792,256]{1,0:T(8,128)S(1)} custom-call(s32[27]{0:T(128)S(1)} %stack.93.at, bf16[640,256]{1,0:T(8,128)(2,1)S(1)} %get-tuple-element.49.lh, bf16[640,256]{1,0:T(8,128)(2,1)S(1)} %get-tuple-element.50.ll, f32[160,7168]{1,0:T(8,128)S(1)} %get-tuple-element.51.refs_0_.refs_7_, f32[160,7168]{1,0:T(8,128)S(1)} %get-tuple-element.52.refs_1_.refs_8_, ...), custom_call_target="tpu_custom_call" | custom-call | flops 1761607680 | bytes 1835008 | tf_op jit(solution)/shard_map/w_send/pallas_call | solution.py:228
  53.3 0.1 collective-permute-start.9
  53.4 3.2 %w_send.2 = f32[1792,256]{1,0:T(8,128)S(1)} custom-call(s32[27]{0:T(128)S(1)} %stack.93.at, bf16[640,256]{1,0:T(8,128)(2,1)S(1)} %get-tuple-element.49.lh, bf16[640,256]{1,0:T(8,128)(2,1)S(1)} %get-tuple-element.50.ll, f32[160,7168]{1,0:T(8,128)S(1)} %get-tuple-element.51.refs_0_.refs_7_, f32[160,7168]{1,0:T(8,128)S(1)} %get-tuple-element.52.refs_1_.refs_8_, ...), custom_call_target="tpu_custom_call" | custom-call | flops 1761607680 | bytes 1835008 | tf_op jit(solution)/shard_map/w_send/pallas_call | solution.py:228
  56.6 0.6 collective-permute-start.6
  57.1 0.0 collective-permute-done.9.got
  57.2 3.3 %w_keep.3 = (f32[896,256]{1,0:T(8,128)S(1)}, f32[896,256]{1,0:T(8,128)S(1)}) custom-call(s32[27]{0:T(128)S(1)} %stack.93.at, f32[1792,256]{1,0:T(8,128)S(1)} %collective-permute-done.9.got, bf16[640,256]{1,0:T(8,128)(2,1)S(1)} %get-tuple-element.49.lh, bf16[640,256]{1,0:T(8,128)(2,1)S(1)} %get-tuple-element.50.ll, ...), custom_call_target="tpu_custom_call" | custom-call | flops 1761607680 | bytes 1835008 | tf_op jit(solution)/shard_map/w_keep/pallas_call | solution.py:246
  60.4 1.6 collective-permute-start.10
  62.1 3.3 %w_keep.2 = (f32[896,256]{1,0:T(8,128)S(1)}, f32[896,256]{1,0:T(8,128)S(1)}) custom-call(s32[27]{0:T(128)S(1)} %stack.93.at, f32[1792,256]{1,0:T(8,128)S(1)} %collective-permute-done.6.got, bf16[640,256]{1,0:T(8,128)(2,1)S(1)} %get-tuple-element.49.lh, bf16[640,256]{1,0:T(8,128)(2,1)S(1)} %get-tuple-element.50.ll, ...), custom_call_target="tpu_custom_call" | custom-call | flops 1761607680 | bytes 1835008 | tf_op jit(solution)/shard_map/w_keep/pallas_call | solution.py:246
  65.4 1.5 collective-permute-start.7
  66.9 1.3 collective-permute-done.12.refs_1_
  68.3 0.6 collective-permute-start.13
  68.9 0.4 collective-permute-start.14
  69.4 2.5 %collective-permute-start.15 = (f32[128,256]{1,0:T(8,128)S(1)}, f32[128,256]{1,0:T(8,128)S(1)}, u32[]{:S(2)}, u32[]{:S(2)}) collective-permute-start(f32[128,256]{1,0:T(8,128)S(1)} %total.14.refs_0_), channel_id=1, source_target_pairs={{0,24},{4,28},{8,16},{12,20},{16,8},{20,12},{24,0},{28,4},{1,25},{... | collective-permute-start | bytes 393224 | tf_op jit(solution)/shard_map/ppermute | solution.py:556
  71.8 19.6 %collective-permute-done.13.refs_1_ = f32[128,256]{1,0:T(8,128)S(1)} collective-permute-done((f32[128,256]{1,0:T(8,128)S(1)}, f32[128,256]{1,0:T(8,128)S(1)}, u32[]{:S(2)}, u32[]{:S(2)}) %collective-permute-start.13) | collective-permute-done | bytes 131104 | tf_op jit(solution)/shard_map/ppermute | solution.py:556
  91.5 1.7 collective-permute-done.15.refs_3_
  93.2 0.1 collective-permute-start.16
  93.3 0.6 halve.3
  93.9 1.5 collective-permute-start.11
  95.5 0.6 halve.2
  96.1 1.6 collective-permute-start.8
  97.7 13.3 %chol_inverse.1 = (f32[256,256]{1,0:T(8,128)S(1)}, bf16[640,256]{1,0:T(8,128)(2,1)S(1)}, bf16[640,256]{1,0:T(8,128)(2,1)S(1)}) custom-call(s32[27]{0:T(128)S(1)} %stack.93.at, f32[128,256]{1,0:T(8,128)S(1)} %total.15.mine, f32[128,256]{1,0:T(8,128)S(1)} %collective-permute-done.16.beside, f32[640,256]{1,0:T(8,128)S(1)} %get-tuple-element.64.left), custom_call_target="tpu_custom_call" | custom-call | flops 4000000000 | bytes 655360 | tf_op jit(solution)/shard_map/chol_inverse/pallas_call | solution.py:362
  111.0 1.5 right_rows.1
  112.5 0.6 collective-permute-start.20
  113.2 0.5 collective-permute-start.17
  113.7 11.3 %collective-permute-done.20.y = f32[448,256]{1,0:T(8,128)S(1)} collective-permute-done((f32[448,256]{1,0:T(8,128)S(1)}, f32[448,256]{1,0:T(8,128)S(1)}, u32[]{:S(2)}, u32[]{:S(2)}) %collective-permute-start.20) | collective-permute-done | bytes 458784 | tf_op jit(solution)/shard_map/ppermute | solution.py:556
  125.0 0.7 join.3
  125.6 0.1 collective-permute-start.34
  125.7 0.7 join.2
  126.4 0.6 collective-permute-start.33
  126.9 0.5 collective-permute-start.21
  127.5 3.6 %collective-permute-done.23.refs_1_ = f32[8,256]{1,0:T(8,128)S(1)} collective-permute-done((f32[8,256]{1,0:T(8,128)S(1)}, f32[8,256]{1,0:T(8,128)S(1)}, u32[]{:S(2)}, u32[]{:S(2)}) %collective-permute-start.23) | collective-permute-done | bytes 8224 | tf_op jit(solution)/shard_map/ppermute | solution.py:556
  131.1 2.0 %collective-permute-start.24 = (f32[8,256]{1,0:T(8,128)S(1)}, f32[8,256]{1,0:T(8,128)S(1)}, u32[]{:S(2)}, u32[]{:S(2)}) collective-permute-start(f32[8,256]{1,0:T(8,128)S(1)} %total.16.refs_0_), channel_id=1, source_target_pairs={{0,2},{1,3},{2,0},{3,1},{4,6},{5,7},{6,4},{7,5},{8,10},{9,11},{10,... | collective-permute-start | bytes 24584 | tf_op jit(solution)/shard_map/ppermute | solution.py:556
  133.1 2.5 %collective-permute-done.24.refs_1_ = f32[8,256]{1,0:T(8,128)S(1)} collective-permute-done((f32[8,256]{1,0:T(8,128)S(1)}, f32[8,256]{1,0:T(8,128)S(1)}, u32[]{:S(2)}, u32[]{:S(2)}) %collective-permute-start.24) | collective-permute-done | bytes 8224 | tf_op jit(solution)/shard_map/ppermute | solution.py:556
  135.7 1.2 collective-permute-done.25.refs_1_
  136.8 0.6 collective-permute-start.26
  137.4 1.5 collective-permute-start.27
  138.9 1.6 collective-permute-done.26.refs_1_
  140.5 1.5 collective-permute-start.28
  142.0 0.6 collective-permute-start.31
  142.6 2.6 %collective-permute-done.28.refs_3_ = f32[8,256]{1,0:T(8,128)S(1)} collective-permute-done((f32[8,256]{1,0:T(8,128)S(1)}, f32[8,256]{1,0:T(8,128)S(1)}, u32[]{:S(2)}, u32[]{:S(2)}) %collective-permute-start.28) | collective-permute-done | bytes 8224 | tf_op jit(solution)/shard_map/ppermute | solution.py:556
  145.1 0.6 collective-permute-start.29
  145.7 1.4 collective-permute-start.18
  147.2 18.0 %collective-permute-done.18.refs_0_ = f32[384,256]{1,0:T(8,128)S(1)} collective-permute-done((f32[384,256]{1,0:T(8,128)S(1)}, f32[384,256]{1,0:T(8,128)S(1)}, u32[]{:S(2)}, u32[]{:S(2)}) %collective-permute-start.18) | collective-permute-done | bytes 393248 | tf_op jit(solution)/shard_map/ppermute | solution.py:556
  165.2 0.5 collective-permute-start.19
  165.7 0.1 collective-permute-start.32
  165.8 0.4 collective-permute-start.30
  166.2 12.9 %final.3 = (f32[640,6912]{1,0:T(8,128)}, f32[640,6912]{1,0:T(8,128)}, f32[6912,256]{1,0:T(8,128)}) custom-call(s32[27]{0:T(128)S(1)} %stack.93.at, f32[896,256]{1,0:T(8,128)S(1)} %get-tuple-element.75.refs_0_, f32[896,256]{1,0:T(8,128)S(1)} %collective-permute-done.33.refs_1_, f32[896,256]{1,0:T(8,128)S(1)} %get-tuple-element.76.refs_2_, ...), custom_call_target="tpu_custom_call" | custom-call | flops 7046430720 | bytes 18350080 | tf_op jit(solution)/shard_map/final/pallas_call | solution.py:519
  179.1 7.6 %final.4 = (f32[640,6912]{1,0:T(8,128)}, f32[640,6912]{1,0:T(8,128)}, f32[6912,256]{1,0:T(8,128)}) custom-call(s32[27]{0:T(128)S(1)} %stack.93.at, f32[512,256]{1,0:T(8,128)S(1)} %collective-permute-done.29.refs_0_, f32[512,256]{1,0:T(8,128)S(1)} %collective-permute-done.30.refs_1_, ...), custom_call_target="tpu_custom_call", output_to_operand_aliasing={{0}: (11, {}), {1}: (12, {}), {2}: (13, {})} | custom-call | flops 4026531840 | bytes 10485760 | tf_op jit(solution)/shard_map/final/pallas_call | solution.py:519
  186.7 6.5 %final.5 = (f32[640,6912]{1,0:T(8,128)}, f32[640,6912]{1,0:T(8,128)}, f32[6912,256]{1,0:T(8,128)}) custom-call(s32[27]{0:T(128)S(1)} %stack.93.at, f32[384,256]{1,0:T(8,128)S(1)} %collective-permute-done.18.refs_0_, f32[384,256]{1,0:T(8,128)S(1)} %collective-permute-done.19.refs_1_, ...), custom_call_target="tpu_custom_call", output_to_operand_aliasing={{0}: (11, {}), {1}: (12, {}), {2}: (13, {})} | custom-call | flops 3019898880 | bytes 7864320 | tf_op jit(solution)/shard_map/final/pallas_call | solution.py:519
  (34 shorter events, 0.2 us)
Async XLA Ops:
  10.4 13.7 %collective-permute-start.2 = (f32[160,256]{1,0:T(8,128)S(1)}, f32[160,256]{1,0:T(8,128)S(1)}, u32[]{:S(2)}, u32[]{:S(2)}) collective-permute-start(f32[160,256]{1,0:T(8,128)S(1)} %get-tuple-element.48), channel_id=1, source_target_pairs={{0,1},{1,0},{2,3},{3,2},{4,5},{5,4},{6,7},{7,6},{8,9},{9,8},{10,11... | collective-permute-start | bytes 491528 | tf_op jit(solution)/shard_map/ppermute | solution.py:556
  13.5 13.7 %collective-permute-start = (f32[160,256]{1,0:T(8,128)S(1)}, f32[160,256]{1,0:T(8,128)S(1)}, u32[]{:S(2)}, u32[]{:S(2)}) collective-permute-start(f32[160,256]{1,0:T(8,128)S(1)} %get-tuple-element.46), channel_id=1, source_target_pairs={{0,1},{1,0},{2,3},{3,2},{4,5},{5,4},{6,7},{7,6},{8,9},{9,8},{10,11... | collective-permute-start | bytes 491528 | tf_op jit(solution)/shard_map/ppermute | solution.py:556
  24.2 14.8 %collective-permute-start.3 = (f32[160,256]{1,0:T(8,128)S(1)}, f32[160,256]{1,0:T(8,128)S(1)}, u32[]{:S(2)}, u32[]{:S(2)}) collective-permute-start(f32[160,256]{1,0:T(8,128)S(1)} %total.12.refs_0_), channel_id=1, source_target_pairs={{0,2},{1,3},{2,0},{3,1},{4,6},{5,7},{6,4},{7,5},{8,10},{9,11},{10,... | collective-permute-start | bytes 491528 | tf_op jit(solution)/shard_map/ppermute | solution.py:556
  27.2 14.2 %collective-permute-start.1 = (f32[160,256]{1,0:T(8,128)S(1)}, f32[160,256]{1,0:T(8,128)S(1)}, u32[]{:S(2)}, u32[]{:S(2)}) collective-permute-start(f32[160,256]{1,0:T(8,128)S(1)} %total.10.refs_0_), channel_id=1, source_target_pairs={{0,2},{1,3},{2,0},{3,1},{4,6},{5,7},{6,4},{7,5},{8,10},{9,11},{10,... | collective-permute-start | bytes 491528 | tf_op jit(solution)/shard_map/ppermute | solution.py:556
  39.0 7.1 %collective-permute-start.5 = (f32[160,256]{1,0:T(8,128)S(1)}, f32[160,256]{1,0:T(8,128)S(1)}, u32[]{:S(2)}, u32[]{:S(2)}) collective-permute-start(f32[160,256]{1,0:T(8,128)S(1)} %total.13.refs_1_), channel_id=1, source_target_pairs={{0,1},{1,0},{2,3},{3,2},{4,5},{5,4},{6,7},{7,6},{8,9},{9,8},{10,11... | collective-permute-start | bytes 491528 | tf_op jit(solution)/shard_map/ppermute | solution.py:556
  41.5 6.9 %collective-permute-start.4 = (f32[160,256]{1,0:T(8,128)S(1)}, f32[160,256]{1,0:T(8,128)S(1)}, u32[]{:S(2)}, u32[]{:S(2)}) collective-permute-start(f32[160,256]{1,0:T(8,128)S(1)} %total.11.refs_0_), channel_id=1, source_target_pairs={{0,1},{1,0},{2,3},{3,2},{4,5},{5,4},{6,7},{7,6},{8,9},{9,8},{10,11... | collective-permute-start | bytes 491528 | tf_op jit(solution)/shard_map/ppermute | solution.py:556
  53.3 3.9 %collective-permute-start.9 = (f32[1792,256]{1,0:T(8,128)S(1)}, f32[1792,256]{1,0:T(8,128)S(1)}, u32[]{:S(2)}, u32[]{:S(2)}) collective-permute-start(f32[1792,256]{1,0:T(8,128)S(1)} %w_send.3), channel_id=1, source_target_pairs={{0,4},{4,0},{8,12},{12,8},{16,20},{20,16},{24,28},{28,24},{1,5},{5... | collective-permute-start | bytes 5505032 | tf_op jit(solution)/shard_map/ppermute | solution.py:556
  56.6 5.5 %collective-permute-start.6 = (f32[1792,256]{1,0:T(8,128)S(1)}, f32[1792,256]{1,0:T(8,128)S(1)}, u32[]{:S(2)}, u32[]{:S(2)}) collective-permute-start(f32[1792,256]{1,0:T(8,128)S(1)} %w_send.2), channel_id=1, source_target_pairs={{0,4},{4,0},{8,12},{12,8},{16,20},{20,16},{24,28},{28,24},{1,5},{5... | collective-permute-start | bytes 5505032 | tf_op jit(solution)/shard_map/ppermute | solution.py:556
  60.4 32.8 %collective-permute-start.10 = (f32[896,256]{1,0:T(8,128)S(1)}, f32[896,256]{1,0:T(8,128)S(1)}, u32[]{:S(2)}, u32[]{:S(2)}) collective-permute-start(f32[896,256]{1,0:T(8,128)S(1)} %get-tuple-element.59), channel_id=1, source_target_pairs={{0,16},{4,20},{8,24},{12,28},{16,0},{20,4},{24,8},{28,12},{1,17},{... | collective-permute-start | bytes 2752520 | tf_op jit(solution)/shard_map/ppermute | solution.py:556
  65.4 30.1 %collective-permute-start.7 = (f32[896,256]{1,0:T(8,128)S(1)}, f32[896,256]{1,0:T(8,128)S(1)}, u32[]{:S(2)}, u32[]{:S(2)}) collective-permute-start(f32[896,256]{1,0:T(8,128)S(1)} %get-tuple-element.55), channel_id=1, source_target_pairs={{0,8},{4,12},{8,0},{12,4},{16,24},{20,28},{24,16},{28,20},{1,9},{5... | collective-permute-start | bytes 2752520 | tf_op jit(solution)/shard_map/ppermute | solution.py:556
  66.9 1.3 collective-permute-start.12
  68.3 23.2 %collective-permute-start.13 = (f32[128,256]{1,0:T(8,128)S(1)}, f32[128,256]{1,0:T(8,128)S(1)}, u32[]{:S(2)}, u32[]{:S(2)}) collective-permute-start(f32[128,256]{1,0:T(8,128)S(1)} %total.14.refs_0_), channel_id=1, source_target_pairs={{0,8},{4,12},{8,0},{12,4},{16,24},{20,28},{24,16},{28,20},{1,9},{5... | collective-permute-start | bytes 393224 | tf_op jit(solution)/shard_map/ppermute | solution.py:556
  68.9 22.6 %collective-permute-start.14 = (f32[128,256]{1,0:T(8,128)S(1)}, f32[128,256]{1,0:T(8,128)S(1)}, u32[]{:S(2)}, u32[]{:S(2)}) collective-permute-start(f32[128,256]{1,0:T(8,128)S(1)} %total.14.refs_0_), channel_id=1, source_target_pairs={{0,16},{4,20},{8,24},{12,28},{16,0},{20,4},{24,8},{28,12},{1,17},{... | collective-permute-start | bytes 393224 | tf_op jit(solution)/shard_map/ppermute | solution.py:556
  69.4 23.8 %collective-permute-start.15 = (f32[128,256]{1,0:T(8,128)S(1)}, f32[128,256]{1,0:T(8,128)S(1)}, u32[]{:S(2)}, u32[]{:S(2)}) collective-permute-start(f32[128,256]{1,0:T(8,128)S(1)} %total.14.refs_0_), channel_id=1, source_target_pairs={{0,24},{4,28},{8,16},{12,20},{16,8},{20,12},{24,0},{28,4},{1,25},{... | collective-permute-start | bytes 393224 | tf_op jit(solution)/shard_map/ppermute | solution.py:556
  93.2 4.5 %collective-permute-start.16 = (f32[128,256]{1,0:T(8,128)S(1)}, f32[128,256]{1,0:T(8,128)S(1)}, u32[]{:S(2)}, u32[]{:S(2)}) collective-permute-start(f32[128,256]{1,0:T(8,128)S(1)} %total.15.mine), channel_id=1, source_target_pairs={{0,4},{4,0},{8,12},{12,8},{16,20},{20,16},{24,28},{28,24},{1,5},{5... | collective-permute-start | bytes 393224 | tf_op jit(solution)/shard_map/ppermute | solution.py:556
  93.9 17.1 %collective-permute-start.11 = (f32[448,256]{1,0:T(8,128)S(1)}, f32[448,256]{1,0:T(8,128)S(1)}, u32[]{:S(2)}, u32[]{:S(2)}) collective-permute-start(f32[448,256]{1,0:T(8,128)S(1)} %get-tuple-element.61), channel_id=1, source_target_pairs={{0,8},{4,12},{8,0},{12,4},{16,24},{20,28},{24,16},{28,20},{1,9},{5... | collective-permute-start | bytes 1376264 | tf_op jit(solution)/shard_map/ppermute | solution.py:556
  96.1 14.9 %collective-permute-start.8 = (f32[448,256]{1,0:T(8,128)S(1)}, f32[448,256]{1,0:T(8,128)S(1)}, u32[]{:S(2)}, u32[]{:S(2)}) collective-permute-start(f32[448,256]{1,0:T(8,128)S(1)} %get-tuple-element.57), channel_id=1, source_target_pairs={{0,16},{4,20},{8,24},{12,28},{16,0},{20,4},{24,8},{28,12},{1,17},{... | collective-permute-start | bytes 1376264 | tf_op jit(solution)/shard_map/ppermute | solution.py:556
  112.5 12.4 %collective-permute-start.20 = (f32[448,256]{1,0:T(8,128)S(1)}, f32[448,256]{1,0:T(8,128)S(1)}, u32[]{:S(2)}, u32[]{:S(2)}) collective-permute-start(f32[448,256]{1,0:T(8,128)S(1)} %get-tuple-element.68.x), channel_id=1, source_target_pairs={{0,8},{4,12},{8,0},{12,4},{16,24},{20,28},{24,16},{28,20},{1,9},{5... | collective-permute-start | bytes 1376264 | tf_op jit(solution)/shard_map/ppermute | solution.py:556
  113.2 12.6 %collective-permute-start.17 = (f32[448,256]{1,0:T(8,128)S(1)}, f32[448,256]{1,0:T(8,128)S(1)}, u32[]{:S(2)}, u32[]{:S(2)}) collective-permute-start(f32[448,256]{1,0:T(8,128)S(1)} %get-tuple-element.66.x), channel_id=1, source_target_pairs={{0,16},{4,20},{8,24},{12,28},{16,0},{20,4},{24,8},{28,12},{1,17},{... | collective-permute-start | bytes 1376264 | tf_op jit(solution)/shard_map/ppermute | solution.py:556
  125.6 40.1 %collective-permute-start.34 = (f32[896,256]{1,0:T(8,128)S(1)}, f32[896,256]{1,0:T(8,128)S(1)}, u32[]{:S(2)}, u32[]{:S(2)}) collective-permute-start(f32[896,256]{1,0:T(8,128)S(1)} %get-tuple-element.76.refs_2_), channel_id=1, source_target_pairs={{0,4},{4,0},{8,12},{12,8},{16,20},{20,16},{24,28},{28,24},{1,5},{5... | collective-permute-start | bytes 2752520 | tf_op jit(solution)/shard_map/ppermute | solution.py:556
  126.4 39.8 %collective-permute-start.33 = (f32[896,256]{1,0:T(8,128)S(1)}, f32[896,256]{1,0:T(8,128)S(1)}, u32[]{:S(2)}, u32[]{:S(2)}) collective-permute-start(f32[896,256]{1,0:T(8,128)S(1)} %get-tuple-element.75.refs_0_), channel_id=1, source_target_pairs={{0,4},{4,0},{8,12},{12,8},{16,20},{20,16},{24,28},{28,24},{1,5},{5... | collective-permute-start | bytes 2752520 | tf_op jit(solution)/shard_map/ppermute | solution.py:556
  126.9 18.8 %collective-permute-start.21 = (f32[384,256]{1,0:T(8,128)S(1)}, f32[384,256]{1,0:T(8,128)S(1)}, u32[]{:S(2)}, u32[]{:S(2)}) collective-permute-start(f32[384,256]{1,0:T(8,128)S(1)} %get-tuple-element.69), channel_id=1, source_target_pairs={{0,16},{4,20},{8,24},{12,28},{16,0},{20,4},{24,8},{28,12},{1,17},{... | collective-permute-start | bytes 1179656 | tf_op jit(solution)/shard_map/ppermute | solution.py:556
  127.5 3.7 %collective-permute-start.23 = (f32[8,256]{1,0:T(8,128)S(1)}, f32[8,256]{1,0:T(8,128)S(1)}, u32[]{:S(2)}, u32[]{:S(2)}) collective-permute-start(f32[8,256]{1,0:T(8,128)S(1)} %get-tuple-element.70.refs_0_), channel_id=1, source_target_pairs={{0,1},{1,0},{2,3},{3,2},{4,5},{5,4},{6,7},{7,6},{8,9},{9,8},{10,11... | collective-permute-start | bytes 24584 | tf_op jit(solution)/shard_map/ppermute | solution.py:556
  131.1 4.5 %collective-permute-start.24 = (f32[8,256]{1,0:T(8,128)S(1)}, f32[8,256]{1,0:T(8,128)S(1)}, u32[]{:S(2)}, u32[]{:S(2)}) collective-permute-start(f32[8,256]{1,0:T(8,128)S(1)} %total.16.refs_0_), channel_id=1, source_target_pairs={{0,2},{1,3},{2,0},{3,1},{4,6},{5,7},{6,4},{7,5},{8,10},{9,11},{10,... | collective-permute-start | bytes 24584 | tf_op jit(solution)/shard_map/ppermute | solution.py:556
  135.7 1.2 collective-permute-start.25
  136.8 3.7 %collective-permute-start.26 = (f32[8,256]{1,0:T(8,128)S(1)}, f32[8,256]{1,0:T(8,128)S(1)}, u32[]{:S(2)}, u32[]{:S(2)}) collective-permute-start(f32[8,256]{1,0:T(8,128)S(1)} %total.18.refs_0_), channel_id=1, source_target_pairs={{0,8},{4,12},{8,0},{12,4},{16,24},{20,28},{24,16},{28,20},{1,9},{5... | collective-permute-start | bytes 24584 | tf_op jit(solution)/shard_map/ppermute | solution.py:556
  137.4 4.6 %collective-permute-start.27 = (f32[8,256]{1,0:T(8,128)S(1)}, f32[8,256]{1,0:T(8,128)S(1)}, u32[]{:S(2)}, u32[]{:S(2)}) collective-permute-start(f32[8,256]{1,0:T(8,128)S(1)} %total.18.refs_0_), channel_id=1, source_target_pairs={{0,16},{4,20},{8,24},{12,28},{16,0},{20,4},{24,8},{28,12},{1,17},{... | collective-permute-start | bytes 24584 | tf_op jit(solution)/shard_map/ppermute | solution.py:556
  140.5 4.6 %collective-permute-start.28 = (f32[8,256]{1,0:T(8,128)S(1)}, f32[8,256]{1,0:T(8,128)S(1)}, u32[]{:S(2)}, u32[]{:S(2)}) collective-permute-start(f32[8,256]{1,0:T(8,128)S(1)} %total.18.refs_0_), channel_id=1, source_target_pairs={{0,24},{4,28},{8,16},{12,20},{16,8},{20,12},{24,0},{28,4},{1,25},{... | collective-permute-start | bytes 24584 | tf_op jit(solution)/shard_map/ppermute | solution.py:556
  142.0 23.1 %collective-permute-start.31 = (f32[512,256]{1,0:T(8,128)S(1)}, f32[512,256]{1,0:T(8,128)S(1)}, u32[]{:S(2)}, u32[]{:S(2)}) collective-permute-start(f32[512,256]{1,0:T(8,128)S(1)} %get-tuple-element.74), channel_id=1, source_target_pairs={{0,16},{4,20},{8,24},{12,28},{16,0},{20,4},{24,8},{28,12},{1,17},{... | collective-permute-start | bytes 1572872 | tf_op jit(solution)/shard_map/ppermute | solution.py:556
  145.1 20.5 %collective-permute-start.29 = (f32[512,256]{1,0:T(8,128)S(1)}, f32[512,256]{1,0:T(8,128)S(1)}, u32[]{:S(2)}, u32[]{:S(2)}) collective-permute-start(f32[512,256]{1,0:T(8,128)S(1)} %get-tuple-element.73), channel_id=1, source_target_pairs={{0,8},{4,12},{8,0},{12,4},{16,24},{20,28},{24,16},{28,20},{1,9},{5... | collective-permute-start | bytes 1572872 | tf_op jit(solution)/shard_map/ppermute | solution.py:556
  145.7 19.4 %collective-permute-start.18 = (f32[384,256]{1,0:T(8,128)S(1)}, f32[384,256]{1,0:T(8,128)S(1)}, u32[]{:S(2)}, u32[]{:S(2)}) collective-permute-start(f32[384,256]{1,0:T(8,128)S(1)} %get-tuple-element.67), channel_id=1, source_target_pairs={{0,8},{4,12},{8,0},{12,4},{16,24},{20,28},{24,16},{28,20},{1,9},{5... | collective-permute-start | bytes 1179656 | tf_op jit(solution)/shard_map/ppermute | solution.py:556
  165.2 21.5 %collective-permute-start.22 = (f32[384,256]{1,0:T(8,128)S(1)}, f32[384,256]{1,0:T(8,128)S(1)}, u32[]{:S(2)}, u32[]{:S(2)}) collective-permute-start(f32[384,256]{1,0:T(8,128)S(1)} %collective-permute-done.21.refs_2_), channel_id=1, source_target_pairs={{0,4},{4,0},{8,12},{12,8},{16,20},{20,16},{24,28},{28,24},{1,5},{5... | collective-permute-start | bytes 1179656 | tf_op jit(solution)/shard_map/ppermute | solution.py:556
  165.2 21.5 %collective-permute-start.19 = (f32[384,256]{1,0:T(8,128)S(1)}, f32[384,256]{1,0:T(8,128)S(1)}, u32[]{:S(2)}, u32[]{:S(2)}) collective-permute-start(f32[384,256]{1,0:T(8,128)S(1)} %collective-permute-done.18.refs_0_), channel_id=1, source_target_pairs={{0,4},{4,0},{8,12},{12,8},{16,20},{20,16},{24,28},{28,24},{1,5},{5... | collective-permute-start | bytes 1179656 | tf_op jit(solution)/shard_map/ppermute | solution.py:556
  165.7 13.4 %collective-permute-start.32 = (f32[512,256]{1,0:T(8,128)S(1)}, f32[512,256]{1,0:T(8,128)S(1)}, u32[]{:S(2)}, u32[]{:S(2)}) collective-permute-start(f32[512,256]{1,0:T(8,128)S(1)} %collective-permute-done.31.refs_2_), channel_id=1, source_target_pairs={{0,4},{4,0},{8,12},{12,8},{16,20},{20,16},{24,28},{28,24},{1,5},{5... | collective-permute-start | bytes 1572872 | tf_op jit(solution)/shard_map/ppermute | solution.py:556
  165.8 13.3 %collective-permute-start.30 = (f32[512,256]{1,0:T(8,128)S(1)}, f32[512,256]{1,0:T(8,128)S(1)}, u32[]{:S(2)}, u32[]{:S(2)}) collective-permute-start(f32[512,256]{1,0:T(8,128)S(1)} %collective-permute-done.29.refs_0_), channel_id=1, source_target_pairs={{0,4},{4,0},{8,12},{12,8},{16,20},{20,16},{24,28},{28,24},{1,5},{5... | collective-permute-start | bytes 1572872 | tf_op jit(solution)/shard_map/ppermute | solution.py:556
where the time goes:
time: 194 us; the launch traced here: 193 us
  waiting for transfers between devices  83.7 us (43%)
  Pallas kernels  79.2 us (41%)
  starting transfers between devices  29.1 us (15%)
    ppermute x35, waiting for transfers between devices, swap(): return lax.ppermute(x, axis, [(i, i ^ mask) for i in range(n)])  83.7 us
    ppermute x35, starting transfers between devices, swap(): return lax.ppermute(x, axis, [(i, i ^ mask) for i in range(n)])  29.1 us
    pallas_call x3, Pallas kernels, final(): pl.pallas_call(functools.partial(final_kernel, len(buffers), place, group...  26.9 us
    pallas_call x3, Pallas kernels, left_rows(): pl.pallas_call(functools.partial(left_kernel, first, which, part), in_spe...  20.1 us
    pallas_call x1, Pallas kernels, chol_inverse(): pl.pallas_call(functools.partial(chol_kernel, place), in_specs=[SMEM] + [...  13.3 us
    pallas_call x2, Pallas kernels, w_keep(): pl.pallas_call(functools.partial(w_keep_kernel, place), grid_spec=pltpu.P...  6.57 us
    pallas_call x2, Pallas kernels, w_send(): pl.pallas_call(functools.partial(w_send_kernel, place), grid_spec=pltpu.P...  6.36 us
  transfers between devices with their start and end apart: 35, of which 14 were waited for; matrix products, arithmetic and copies ran while one was open for 0% of the time, Pallas kernels for 29%

commit v1 on v0

--- a/solution.py
+++ b/solution.py
@@ -54,7 +54,7 @@
     return LANES * max(k for k in range(1, 9) if blocks % k == 0)
 
 
-DEPTH = 4
+FIRST_DEPTH, LATER_DEPTH = 6, 9
 
 
 def left_kernel(first, which, part, at, g, m, *refs):
@@ -116,6 +116,7 @@
     wide = column_block(cols)
     n = rows // 2 if first else rows // (2 * parts)
     outs = parts if first else 1
+    depth = FIRST_DEPTH if first else LATER_DEPTH
     terms = [pltpu.VMEM((cols, rank), BF16)] * 2 if first else []
     return pl.pallas_call(
         functools.partial(left_kernel, first, which, part),
@@ -124,9 +125,9 @@
         out_shape=[pltpu.VMEM((n, padded), F32)]
         + terms
         + [jax.ShapeDtypeStruct((rows // (2 * parts), rank), F32)] * outs,
-        scratch_shapes=[pltpu.VMEM((DEPTH, n, wide), F32)] * 2
-        + ([pltpu.VMEM((DEPTH, wide, rank), F32)] if first else [])
-        + [pltpu.SemaphoreType.DMA((3 if first else 2, DEPTH))],
+        scratch_shapes=[pltpu.VMEM((depth, n, wide), F32)] * 2
+        + ([pltpu.VMEM((depth, wide, rank), F32)] if first else [])
+        + [pltpu.SemaphoreType.DMA((3 if first else 2, depth))],
         compiler_params=params(34 if first else 30),
         cost_estimate=cost(6 * n * cols * rank, 4 * (2 * n * cols + cols * rank)),
         name="left_rows",

time: 194 us -> 194 us (level)
  no operation moved by 1% of the time
where the time goes in v1:
time: 194 us
  waiting for transfers between devices  83.8 us (43%)
  Pallas kernels  79.5 us (41%)
  starting transfers between devices  29.1 us (15%)
    ppermute x35, waiting for transfers between devices, swap(): return lax.ppermute(x, axis, [(i, i ^ mask) for i in range(n)])  83.8 us
    ppermute x35, starting transfers between devices, swap(): return lax.ppermute(x, axis, [(i, i ^ mask) for i in range(n)])  29.1 us
    pallas_call x3, Pallas kernels, final(): pl.pallas_call(functools.partial(final_kernel, len(buffers), place, group...  26.9 us
    pallas_call x3, Pallas kernels, left_rows(): pl.pallas_call(functools.partial(left_kernel, first, which, part), in_spe...  20.4 us
    pallas_call x1, Pallas kernels, chol_inverse(): pl.pallas_call(functools.partial(chol_kernel, place), in_specs=[SMEM] + [...  13.3 us
    pallas_call x2, Pallas kernels, w_keep(): pl.pallas_call(functools.partial(w_keep_kernel, place), grid_spec=pltpu.P...  6.57 us
    pallas_call x2, Pallas kernels, w_send(): pl.pallas_call(functools.partial(w_send_kernel, place), grid_spec=pltpu.P...  6.36 us
  transfers between devices with their start and end apart: 35, of which 14 were waited for; matrix products, arithmetic and copies ran while one was open for 0% of the time, Pallas kernels for 29%

profile of v1, /device:TPU:0, one launch (start us, length us, event | category | flops | bytes accessed | tf_op | source)
XLA Modules:
  0.0 193.6 jit_solution(9383873244689182831)
XLA Ops:
  0.7 0.1 stack.93.at
  0.8 9.7 %left_rows.3 = (f32[320,7168]{1,0:T(8,128)S(1)}, bf16[6912,256]{1,0:T(8,128)(2,1)S(1)}, bf16[6912,256]{1,0:T(8,128)(2,1)S(1)}, f32[160,256]{1,0:T(8,128)S(1)}, f32[160,256]{1,0:T(8,128)S(1)}) custom-call(s32[27]{0:T(128)S(1)} %stack.93.at, f32[640,6912]{1,0:T(8,128)} %g.5, f32[640,6912]{1,0:T(8,128)} %m.5, f32[6912,256]{1,0:T(8,128)} %refs_0_.1), custom_call_target="tpu_custom_call" | custom-call | flops 3397386240 | bytes 24772608 | tf_op jit(solution)/shard_map/left_rows/pallas_call | solution.py:121
  10.5 3.1 %collective-permute-start.2 = (f32[160,256]{1,0:T(8,128)S(1)}, f32[160,256]{1,0:T(8,128)S(1)}, u32[]{:S(2)}, u32[]{:S(2)}) collective-permute-start(f32[160,256]{1,0:T(8,128)S(1)} %get-tuple-element.48), channel_id=1, source_target_pairs={{0,1},{1,0},{2,3},{3,2},{4,5},{5,4},{6,7},{7,6},{8,9},{9,8},{10,11... | collective-permute-start | bytes 491528 | tf_op jit(solution)/shard_map/ppermute | solution.py:557
  13.6 0.1 collective-permute-start
  13.6 5.4 %left_rows.5 = (f32[160,7168]{1,0:T(8,128)S(1)}, f32[160,256]{1,0:T(8,128)S(1)}) custom-call(s32[27]{0:T(128)S(1)} %stack.93.at, f32[640,6912]{1,0:T(8,128)} %g.5, f32[640,6912]{1,0:T(8,128)} %m.5, bf16[6912,256]{1,0:T(8,128)(2,1)S(1)} %get-tuple-element.43.refs_0_, bf16[6912,256]{1,0:T(8,128)(2,1)S(1)} %get-tuple-element.44.refs_1_), custom_call_target="tpu_custom_call" | custom-call | flops 1698693120 | bytes 15925248 | tf_op jit(solution)/shard_map/left_rows/pallas_call | solution.py:121
  19.0 5.4 %left_rows.4 = (f32[160,7168]{1,0:T(8,128)S(1)}, f32[160,256]{1,0:T(8,128)S(1)}) custom-call(s32[27]{0:T(128)S(1)} %stack.93.at, f32[640,6912]{1,0:T(8,128)} %g.5, f32[640,6912]{1,0:T(8,128)} %m.5, bf16[6912,256]{1,0:T(8,128)(2,1)S(1)} %get-tuple-element.43.refs_0_, bf16[6912,256]{1,0:T(8,128)(2,1)S(1)} %get-tuple-element.44.refs_1_), custom_call_target="tpu_custom_call" | custom-call | flops 1698693120 | bytes 15925248 | tf_op jit(solution)/shard_map/left_rows/pallas_call | solution.py:121
  24.4 3.0 %collective-permute-start.3 = (f32[160,256]{1,0:T(8,128)S(1)}, f32[160,256]{1,0:T(8,128)S(1)}, u32[]{:S(2)}, u32[]{:S(2)}) collective-permute-start(f32[160,256]{1,0:T(8,128)S(1)} %total.12.refs_0_), channel_id=1, source_target_pairs={{0,2},{1,3},{2,0},{3,1},{4,6},{5,7},{6,4},{7,5},{8,10},{9,11},{10,... | collective-permute-start | bytes 491528 | tf_op jit(solution)/shard_map/ppermute | solution.py:557
  27.5 0.1 collective-permute-start.1
  27.6 11.7 %collective-permute-done.3.refs_1_ = f32[160,256]{1,0:T(8,128)S(1)} collective-permute-done((f32[160,256]{1,0:T(8,128)S(1)}, f32[160,256]{1,0:T(8,128)S(1)}, u32[]{:S(2)}, u32[]{:S(2)}) %collective-permute-start.3) | collective-permute-done | bytes 163872 | tf_op jit(solution)/shard_map/ppermute | solution.py:557
  39.3 0.1 collective-permute-start.5
  39.4 2.3 %collective-permute-done.1.refs_1_ = f32[160,256]{1,0:T(8,128)S(1)} collective-permute-done((f32[160,256]{1,0:T(8,128)S(1)}, f32[160,256]{1,0:T(8,128)S(1)}, u32[]{:S(2)}, u32[]{:S(2)}) %collective-permute-start.1) | collective-permute-done | bytes 163872 | tf_op jit(solution)/shard_map/ppermute | solution.py:557
  41.7 0.7 collective-permute-start.4
  42.4 4.0 %collective-permute-done.5.refs_3_ = f32[160,256]{1,0:T(8,128)S(1)} collective-permute-done((f32[160,256]{1,0:T(8,128)S(1)}, f32[160,256]{1,0:T(8,128)S(1)}, u32[]{:S(2)}, u32[]{:S(2)}) %collective-permute-start.5) | collective-permute-done | bytes 163872 | tf_op jit(solution)/shard_map/ppermute | solution.py:557
  46.4 2.2 %collective-permute-done.4.refs_2_ = f32[160,256]{1,0:T(8,128)S(1)} collective-permute-done((f32[160,256]{1,0:T(8,128)S(1)}, f32[160,256]{1,0:T(8,128)S(1)}, u32[]{:S(2)}, u32[]{:S(2)}) %collective-permute-start.4) | collective-permute-done | bytes 163872 | tf_op jit(solution)/shard_map/ppermute | solution.py:557
  48.6 1.7 gram_of.1
  50.4 3.2 %w_send.3 = f32[1792,256]{1,0:T(8,128)S(1)} custom-call(s32[27]{0:T(128)S(1)} %stack.93.at, bf16[640,256]{1,0:T(8,128)(2,1)S(1)} %get-tuple-element.49.lh, bf16[640,256]{1,0:T(8,128)(2,1)S(1)} %get-tuple-element.50.ll, f32[160,7168]{1,0:T(8,128)S(1)} %get-tuple-element.51.refs_0_.refs_7_, f32[160,7168]{1,0:T(8,128)S(1)} %get-tuple-element.52.refs_1_.refs_8_, ...), custom_call_target="tpu_custom_call" | custom-call | flops 1761607680 | bytes 1835008 | tf_op jit(solution)/shard_map/w_send/pallas_call | solution.py:229
  53.6 0.1 collective-permute-start.9
  53.6 3.2 %w_send.2 = f32[1792,256]{1,0:T(8,128)S(1)} custom-call(s32[27]{0:T(128)S(1)} %stack.93.at, bf16[640,256]{1,0:T(8,128)(2,1)S(1)} %get-tuple-element.49.lh, bf16[640,256]{1,0:T(8,128)(2,1)S(1)} %get-tuple-element.50.ll, f32[160,7168]{1,0:T(8,128)S(1)} %get-tuple-element.51.refs_0_.refs_7_, f32[160,7168]{1,0:T(8,128)S(1)} %get-tuple-element.52.refs_1_.refs_8_, ...), custom_call_target="tpu_custom_call" | custom-call | flops 1761607680 | bytes 1835008 | tf_op jit(solution)/shard_map/w_send/pallas_call | solution.py:229
  56.8 0.5 collective-permute-start.6
  57.4 0.0 collective-permute-done.9.got
  57.4 3.3 %w_keep.3 = (f32[896,256]{1,0:T(8,128)S(1)}, f32[896,256]{1,0:T(8,128)S(1)}) custom-call(s32[27]{0:T(128)S(1)} %stack.93.at, f32[1792,256]{1,0:T(8,128)S(1)} %collective-permute-done.9.got, bf16[640,256]{1,0:T(8,128)(2,1)S(1)} %get-tuple-element.49.lh, bf16[640,256]{1,0:T(8,128)(2,1)S(1)} %get-tuple-element.50.ll, ...), custom_call_target="tpu_custom_call" | custom-call | flops 1761607680 | bytes 1835008 | tf_op jit(solution)/shard_map/w_keep/pallas_call | solution.py:247
  60.7 1.6 collective-permute-start.10
  62.3 3.3 %w_keep.2 = (f32[896,256]{1,0:T(8,128)S(1)}, f32[896,256]{1,0:T(8,128)S(1)}) custom-call(s32[27]{0:T(128)S(1)} %stack.93.at, f32[1792,256]{1,0:T(8,128)S(1)} %collective-permute-done.6.got, bf16[640,256]{1,0:T(8,128)(2,1)S(1)} %get-tuple-element.49.lh, bf16[640,256]{1,0:T(8,128)(2,1)S(1)} %get-tuple-element.50.ll, ...), custom_call_target="tpu_custom_call" | custom-call | flops 1761607680 | bytes 1835008 | tf_op jit(solution)/shard_map/w_keep/pallas_call | solution.py:247
  65.6 1.6 collective-permute-start.7
  67.2 1.3 collective-permute-done.12.refs_1_
  68.6 0.6 collective-permute-start.13
  69.2 0.4 collective-permute-start.14
  69.6 2.5 %collective-permute-start.15 = (f32[128,256]{1,0:T(8,128)S(1)}, f32[128,256]{1,0:T(8,128)S(1)}, u32[]{:S(2)}, u32[]{:S(2)}) collective-permute-start(f32[128,256]{1,0:T(8,128)S(1)} %total.14.refs_0_), channel_id=1, source_target_pairs={{0,24},{4,28},{8,16},{12,20},{16,8},{20,12},{24,0},{28,4},{1,25},{... | collective-permute-start | bytes 393224 | tf_op jit(solution)/shard_map/ppermute | solution.py:557
  72.1 19.6 %collective-permute-done.13.refs_1_ = f32[128,256]{1,0:T(8,128)S(1)} collective-permute-done((f32[128,256]{1,0:T(8,128)S(1)}, f32[128,256]{1,0:T(8,128)S(1)}, u32[]{:S(2)}, u32[]{:S(2)}) %collective-permute-start.13) | collective-permute-done | bytes 131104 | tf_op jit(solution)/shard_map/ppermute | solution.py:557
  91.7 1.7 collective-permute-done.15.refs_3_
  93.4 0.1 collective-permute-start.16
  93.5 0.6 halve.3
  94.2 1.6 collective-permute-start.11
  95.8 0.6 halve.2
  96.4 1.6 collective-permute-start.8
  98.0 13.3 %chol_inverse.1 = (f32[256,256]{1,0:T(8,128)S(1)}, bf16[640,256]{1,0:T(8,128)(2,1)S(1)}, bf16[640,256]{1,0:T(8,128)(2,1)S(1)}) custom-call(s32[27]{0:T(128)S(1)} %stack.93.at, f32[128,256]{1,0:T(8,128)S(1)} %total.15.mine, f32[128,256]{1,0:T(8,128)S(1)} %collective-permute-done.16.beside, f32[640,256]{1,0:T(8,128)S(1)} %get-tuple-element.64.left), custom_call_target="tpu_custom_call" | custom-call | flops 4000000000 | bytes 655360 | tf_op jit(solution)/shard_map/chol_inverse/pallas_call | solution.py:363
  111.3 1.5 right_rows.1
  112.8 0.6 collective-permute-start.20
  113.4 0.5 collective-permute-start.17
  113.9 11.3 %collective-permute-done.20.y = f32[448,256]{1,0:T(8,128)S(1)} collective-permute-done((f32[448,256]{1,0:T(8,128)S(1)}, f32[448,256]{1,0:T(8,128)S(1)}, u32[]{:S(2)}, u32[]{:S(2)}) %collective-permute-start.20) | collective-permute-done | bytes 458784 | tf_op jit(solution)/shard_map/ppermute | solution.py:557
  125.2 0.7 join.3
  125.9 0.1 collective-permute-start.34
  126.0 0.7 join.2
  126.7 0.6 collective-permute-start.33
  127.2 0.5 collective-permute-start.21
  127.7 3.6 %collective-permute-done.23.refs_1_ = f32[8,256]{1,0:T(8,128)S(1)} collective-permute-done((f32[8,256]{1,0:T(8,128)S(1)}, f32[8,256]{1,0:T(8,128)S(1)}, u32[]{:S(2)}, u32[]{:S(2)}) %collective-permute-start.23) | collective-permute-done | bytes 8224 | tf_op jit(solution)/shard_map/ppermute | solution.py:557
  131.4 2.0 %collective-permute-start.24 = (f32[8,256]{1,0:T(8,128)S(1)}, f32[8,256]{1,0:T(8,128)S(1)}, u32[]{:S(2)}, u32[]{:S(2)}) collective-permute-start(f32[8,256]{1,0:T(8,128)S(1)} %total.16.refs_0_), channel_id=1, source_target_pairs={{0,2},{1,3},{2,0},{3,1},{4,6},{5,7},{6,4},{7,5},{8,10},{9,11},{10,... | collective-permute-start | bytes 24584 | tf_op jit(solution)/shard_map/ppermute | solution.py:557
  133.4 2.5 %collective-permute-done.24.refs_1_ = f32[8,256]{1,0:T(8,128)S(1)} collective-permute-done((f32[8,256]{1,0:T(8,128)S(1)}, f32[8,256]{1,0:T(8,128)S(1)}, u32[]{:S(2)}, u32[]{:S(2)}) %collective-permute-start.24) | collective-permute-done | bytes 8224 | tf_op jit(solution)/shard_map/ppermute | solution.py:557
  135.9 1.2 collective-permute-done.25.refs_1_
  137.1 0.6 collective-permute-start.26
  137.7 1.5 collective-permute-start.27
  139.2 1.6 collective-permute-done.26.refs_1_
  140.8 1.5 collective-permute-start.28
  142.3 0.6 collective-permute-start.31
  142.9 2.6 %collective-permute-done.28.refs_3_ = f32[8,256]{1,0:T(8,128)S(1)} collective-permute-done((f32[8,256]{1,0:T(8,128)S(1)}, f32[8,256]{1,0:T(8,128)S(1)}, u32[]{:S(2)}, u32[]{:S(2)}) %collective-permute-start.28) | collective-permute-done | bytes 8224 | tf_op jit(solution)/shard_map/ppermute | solution.py:557
  145.4 0.6 collective-permute-start.29
  146.0 1.5 collective-permute-start.18
  147.5 18.0 %collective-permute-done.18.refs_0_ = f32[384,256]{1,0:T(8,128)S(1)} collective-permute-done((f32[384,256]{1,0:T(8,128)S(1)}, f32[384,256]{1,0:T(8,128)S(1)}, u32[]{:S(2)}, u32[]{:S(2)}) %collective-permute-start.18) | collective-permute-done | bytes 393248 | tf_op jit(solution)/shard_map/ppermute | solution.py:557
  165.5 0.5 collective-permute-start.19
  166.0 0.1 collective-permute-start.32
  166.0 0.4 collective-permute-start.30
  166.5 12.9 %final.3 = (f32[640,6912]{1,0:T(8,128)}, f32[640,6912]{1,0:T(8,128)}, f32[6912,256]{1,0:T(8,128)}) custom-call(s32[27]{0:T(128)S(1)} %stack.93.at, f32[896,256]{1,0:T(8,128)S(1)} %get-tuple-element.75.refs_0_, f32[896,256]{1,0:T(8,128)S(1)} %collective-permute-done.33.refs_1_, f32[896,256]{1,0:T(8,128)S(1)} %get-tuple-element.76.refs_2_, ...), custom_call_target="tpu_custom_call" | custom-call | flops 7046430720 | bytes 18350080 | tf_op jit(solution)/shard_map/final/pallas_call | solution.py:520
  179.4 7.6 %final.4 = (f32[640,6912]{1,0:T(8,128)}, f32[640,6912]{1,0:T(8,128)}, f32[6912,256]{1,0:T(8,128)}) custom-call(s32[27]{0:T(128)S(1)} %stack.93.at, f32[512,256]{1,0:T(8,128)S(1)} %collective-permute-done.29.refs_0_, f32[512,256]{1,0:T(8,128)S(1)} %collective-permute-done.30.refs_1_, ...), custom_call_target="tpu_custom_call", output_to_operand_aliasing={{0}: (11, {}), {1}: (12, {}), {2}: (13, {})} | custom-call | flops 4026531840 | bytes 10485760 | tf_op jit(solution)/shard_map/final/pallas_call | solution.py:520
  187.0 6.5 %final.5 = (f32[640,6912]{1,0:T(8,128)}, f32[640,6912]{1,0:T(8,128)}, f32[6912,256]{1,0:T(8,128)}) custom-call(s32[27]{0:T(128)S(1)} %stack.93.at, f32[384,256]{1,0:T(8,128)S(1)} %collective-permute-done.18.refs_0_, f32[384,256]{1,0:T(8,128)S(1)} %collective-permute-done.19.refs_1_, ...), custom_call_target="tpu_custom_call", output_to_operand_aliasing={{0}: (11, {}), {1}: (12, {}), {2}: (13, {})} | custom-call | flops 3019898880 | bytes 7864320 | tf_op jit(solution)/shard_map/final/pallas_call | solution.py:520
  (34 shorter events, 0.2 us)
Async XLA Ops:
  10.5 13.9 %collective-permute-start.2 = (f32[160,256]{1,0:T(8,128)S(1)}, f32[160,256]{1,0:T(8,128)S(1)}, u32[]{:S(2)}, u32[]{:S(2)}) collective-permute-start(f32[160,256]{1,0:T(8,128)S(1)} %get-tuple-element.48), channel_id=1, source_target_pairs={{0,1},{1,0},{2,3},{3,2},{4,5},{5,4},{6,7},{7,6},{8,9},{9,8},{10,11... | collective-permute-start | bytes 491528 | tf_op jit(solution)/shard_map/ppermute | solution.py:557
  13.6 13.9 %collective-permute-start = (f32[160,256]{1,0:T(8,128)S(1)}, f32[160,256]{1,0:T(8,128)S(1)}, u32[]{:S(2)}, u32[]{:S(2)}) collective-permute-start(f32[160,256]{1,0:T(8,128)S(1)} %get-tuple-element.46), channel_id=1, source_target_pairs={{0,1},{1,0},{2,3},{3,2},{4,5},{5,4},{6,7},{7,6},{8,9},{9,8},{10,11... | collective-permute-start | bytes 491528 | tf_op jit(solution)/shard_map/ppermute | solution.py:557
  24.4 14.8 %collective-permute-start.3 = (f32[160,256]{1,0:T(8,128)S(1)}, f32[160,256]{1,0:T(8,128)S(1)}, u32[]{:S(2)}, u32[]{:S(2)}) collective-permute-start(f32[160,256]{1,0:T(8,128)S(1)} %total.12.refs_0_), channel_id=1, source_target_pairs={{0,2},{1,3},{2,0},{3,1},{4,6},{5,7},{6,4},{7,5},{8,10},{9,11},{10,... | collective-permute-start | bytes 491528 | tf_op jit(solution)/shard_map/ppermute | solution.py:557
  27.5 14.3 %collective-permute-start.1 = (f32[160,256]{1,0:T(8,128)S(1)}, f32[160,256]{1,0:T(8,128)S(1)}, u32[]{:S(2)}, u32[]{:S(2)}) collective-permute-start(f32[160,256]{1,0:T(8,128)S(1)} %total.10.refs_0_), channel_id=1, source_target_pairs={{0,2},{1,3},{2,0},{3,1},{4,6},{5,7},{6,4},{7,5},{8,10},{9,11},{10,... | collective-permute-start | bytes 491528 | tf_op jit(solution)/shard_map/ppermute | solution.py:557
  39.3 7.1 %collective-permute-start.5 = (f32[160,256]{1,0:T(8,128)S(1)}, f32[160,256]{1,0:T(8,128)S(1)}, u32[]{:S(2)}, u32[]{:S(2)}) collective-permute-start(f32[160,256]{1,0:T(8,128)S(1)} %total.13.refs_1_), channel_id=1, source_target_pairs={{0,1},{1,0},{2,3},{3,2},{4,5},{5,4},{6,7},{7,6},{8,9},{9,8},{10,11... | collective-permute-start | bytes 491528 | tf_op jit(solution)/shard_map/ppermute | solution.py:557
  41.7 6.9 %collective-permute-start.4 = (f32[160,256]{1,0:T(8,128)S(1)}, f32[160,256]{1,0:T(8,128)S(1)}, u32[]{:S(2)}, u32[]{:S(2)}) collective-permute-start(f32[160,256]{1,0:T(8,128)S(1)} %total.11.refs_0_), channel_id=1, source_target_pairs={{0,1},{1,0},{2,3},{3,2},{4,5},{5,4},{6,7},{7,6},{8,9},{9,8},{10,11... | collective-permute-start | bytes 491528 | tf_op jit(solution)/shard_map/ppermute | solution.py:557
  53.6 3.9 %collective-permute-start.9 = (f32[1792,256]{1,0:T(8,128)S(1)}, f32[1792,256]{1,0:T(8,128)S(1)}, u32[]{:S(2)}, u32[]{:S(2)}) collective-permute-start(f32[1792,256]{1,0:T(8,128)S(1)} %w_send.3), channel_id=1, source_target_pairs={{0,4},{4,0},{8,12},{12,8},{16,20},{20,16},{24,28},{28,24},{1,5},{5... | collective-permute-start | bytes 5505032 | tf_op jit(solution)/shard_map/ppermute | solution.py:557
  56.8 5.5 %collective-permute-start.6 = (f32[1792,256]{1,0:T(8,128)S(1)}, f32[1792,256]{1,0:T(8,128)S(1)}, u32[]{:S(2)}, u32[]{:S(2)}) collective-permute-start(f32[1792,256]{1,0:T(8,128)S(1)} %w_send.2), channel_id=1, source_target_pairs={{0,4},{4,0},{8,12},{12,8},{16,20},{20,16},{24,28},{28,24},{1,5},{5... | collective-permute-start | bytes 5505032 | tf_op jit(solution)/shard_map/ppermute | solution.py:557
  60.7 32.8 %collective-permute-start.10 = (f32[896,256]{1,0:T(8,128)S(1)}, f32[896,256]{1,0:T(8,128)S(1)}, u32[]{:S(2)}, u32[]{:S(2)}) collective-permute-start(f32[896,256]{1,0:T(8,128)S(1)} %get-tuple-element.59), channel_id=1, source_target_pairs={{0,16},{4,20},{8,24},{12,28},{16,0},{20,4},{24,8},{28,12},{1,17},{... | collective-permute-start | bytes 2752520 | tf_op jit(solution)/shard_map/ppermute | solution.py:557
  65.6 30.1 %collective-permute-start.7 = (f32[896,256]{1,0:T(8,128)S(1)}, f32[896,256]{1,0:T(8,128)S(1)}, u32[]{:S(2)}, u32[]{:S(2)}) collective-permute-start(f32[896,256]{1,0:T(8,128)S(1)} %get-tuple-element.55), channel_id=1, source_target_pairs={{0,8},{4,12},{8,0},{12,4},{16,24},{20,28},{24,16},{28,20},{1,9},{5... | collective-permute-start | bytes 2752520 | tf_op jit(solution)/shard_map/ppermute | solution.py:557
  67.2 1.3 collective-permute-start.12
  68.6 23.2 %collective-permute-start.13 = (f32[128,256]{1,0:T(8,128)S(1)}, f32[128,256]{1,0:T(8,128)S(1)}, u32[]{:S(2)}, u32[]{:S(2)}) collective-permute-start(f32[128,256]{1,0:T(8,128)S(1)} %total.14.refs_0_), channel_id=1, source_target_pairs={{0,8},{4,12},{8,0},{12,4},{16,24},{20,28},{24,16},{28,20},{1,9},{5... | collective-permute-start | bytes 393224 | tf_op jit(solution)/shard_map/ppermute | solution.py:557
  69.2 22.6 %collective-permute-start.14 = (f32[128,256]{1,0:T(8,128)S(1)}, f32[128,256]{1,0:T(8,128)S(1)}, u32[]{:S(2)}, u32[]{:S(2)}) collective-permute-start(f32[128,256]{1,0:T(8,128)S(1)} %total.14.refs_0_), channel_id=1, source_target_pairs={{0,16},{4,20},{8,24},{12,28},{16,0},{20,4},{24,8},{28,12},{1,17},{... | collective-permute-start | bytes 393224 | tf_op jit(solution)/shard_map/ppermute | solution.py:557
  69.6 23.8 %collective-permute-start.15 = (f32[128,256]{1,0:T(8,128)S(1)}, f32[128,256]{1,0:T(8,128)S(1)}, u32[]{:S(2)}, u32[]{:S(2)}) collective-permute-start(f32[128,256]{1,0:T(8,128)S(1)} %total.14.refs_0_), channel_id=1, source_target_pairs={{0,24},{4,28},{8,16},{12,20},{16,8},{20,12},{24,0},{28,4},{1,25},{... | collective-permute-start | bytes 393224 | tf_op jit(solution)/shard_map/ppermute | solution.py:557
  93.4 4.5 %collective-permute-start.16 = (f32[128,256]{1,0:T(8,128)S(1)}, f32[128,256]{1,0:T(8,128)S(1)}, u32[]{:S(2)}, u32[]{:S(2)}) collective-permute-start(f32[128,256]{1,0:T(8,128)S(1)} %total.15.mine), channel_id=1, source_target_pairs={{0,4},{4,0},{8,12},{12,8},{16,20},{20,16},{24,28},{28,24},{1,5},{5... | collective-permute-start | bytes 393224 | tf_op jit(solution)/shard_map/ppermute | solution.py:557
  94.2 17.1 %collective-permute-start.11 = (f32[448,256]{1,0:T(8,128)S(1)}, f32[448,256]{1,0:T(8,128)S(1)}, u32[]{:S(2)}, u32[]{:S(2)}) collective-permute-start(f32[448,256]{1,0:T(8,128)S(1)} %get-tuple-element.61), channel_id=1, source_target_pairs={{0,8},{4,12},{8,0},{12,4},{16,24},{20,28},{24,16},{28,20},{1,9},{5... | collective-permute-start | bytes 1376264 | tf_op jit(solution)/shard_map/ppermute | solution.py:557
  96.4 14.9 %collective-permute-start.8 = (f32[448,256]{1,0:T(8,128)S(1)}, f32[448,256]{1,0:T(8,128)S(1)}, u32[]{:S(2)}, u32[]{:S(2)}) collective-permute-start(f32[448,256]{1,0:T(8,128)S(1)} %get-tuple-element.57), channel_id=1, source_target_pairs={{0,16},{4,20},{8,24},{12,28},{16,0},{20,4},{24,8},{28,12},{1,17},{... | collective-permute-start | bytes 1376264 | tf_op jit(solution)/shard_map/ppermute | solution.py:557
  112.8 12.4 %collective-permute-start.20 = (f32[448,256]{1,0:T(8,128)S(1)}, f32[448,256]{1,0:T(8,128)S(1)}, u32[]{:S(2)}, u32[]{:S(2)}) collective-permute-start(f32[448,256]{1,0:T(8,128)S(1)} %get-tuple-element.68.x), channel_id=1, source_target_pairs={{0,8},{4,12},{8,0},{12,4},{16,24},{20,28},{24,16},{28,20},{1,9},{5... | collective-permute-start | bytes 1376264 | tf_op jit(solution)/shard_map/ppermute | solution.py:557
  113.4 12.6 %collective-permute-start.17 = (f32[448,256]{1,0:T(8,128)S(1)}, f32[448,256]{1,0:T(8,128)S(1)}, u32[]{:S(2)}, u32[]{:S(2)}) collective-permute-start(f32[448,256]{1,0:T(8,128)S(1)} %get-tuple-element.66.x), channel_id=1, source_target_pairs={{0,16},{4,20},{8,24},{12,28},{16,0},{20,4},{24,8},{28,12},{1,17},{... | collective-permute-start | bytes 1376264 | tf_op jit(solution)/shard_map/ppermute | solution.py:557
  125.9 40.1 %collective-permute-start.34 = (f32[896,256]{1,0:T(8,128)S(1)}, f32[896,256]{1,0:T(8,128)S(1)}, u32[]{:S(2)}, u32[]{:S(2)}) collective-permute-start(f32[896,256]{1,0:T(8,128)S(1)} %get-tuple-element.76.refs_2_), channel_id=1, source_target_pairs={{0,4},{4,0},{8,12},{12,8},{16,20},{20,16},{24,28},{28,24},{1,5},{5... | collective-permute-start | bytes 2752520 | tf_op jit(solution)/shard_map/ppermute | solution.py:557
  126.7 39.8 %collective-permute-start.33 = (f32[896,256]{1,0:T(8,128)S(1)}, f32[896,256]{1,0:T(8,128)S(1)}, u32[]{:S(2)}, u32[]{:S(2)}) collective-permute-start(f32[896,256]{1,0:T(8,128)S(1)} %get-tuple-element.75.refs_0_), channel_id=1, source_target_pairs={{0,4},{4,0},{8,12},{12,8},{16,20},{20,16},{24,28},{28,24},{1,5},{5... | collective-permute-start | bytes 2752520 | tf_op jit(solution)/shard_map/ppermute | solution.py:557
  127.2 18.8 %collective-permute-start.21 = (f32[384,256]{1,0:T(8,128)S(1)}, f32[384,256]{1,0:T(8,128)S(1)}, u32[]{:S(2)}, u32[]{:S(2)}) collective-permute-start(f32[384,256]{1,0:T(8,128)S(1)} %get-tuple-element.69), channel_id=1, source_target_pairs={{0,16},{4,20},{8,24},{12,28},{16,0},{20,4},{24,8},{28,12},{1,17},{... | collective-permute-start | bytes 1179656 | tf_op jit(solution)/shard_map/ppermute | solution.py:557
  127.7 3.7 %collective-permute-start.23 = (f32[8,256]{1,0:T(8,128)S(1)}, f32[8,256]{1,0:T(8,128)S(1)}, u32[]{:S(2)}, u32[]{:S(2)}) collective-permute-start(f32[8,256]{1,0:T(8,128)S(1)} %get-tuple-element.70.refs_0_), channel_id=1, source_target_pairs={{0,1},{1,0},{2,3},{3,2},{4,5},{5,4},{6,7},{7,6},{8,9},{9,8},{10,11... | collective-permute-start | bytes 24584 | tf_op jit(solution)/shard_map/ppermute | solution.py:557
  131.4 4.5 %collective-permute-start.24 = (f32[8,256]{1,0:T(8,128)S(1)}, f32[8,256]{1,0:T(8,128)S(1)}, u32[]{:S(2)}, u32[]{:S(2)}) collective-permute-start(f32[8,256]{1,0:T(8,128)S(1)} %total.16.refs_0_), channel_id=1, source_target_pairs={{0,2},{1,3},{2,0},{3,1},{4,6},{5,7},{6,4},{7,5},{8,10},{9,11},{10,... | collective-permute-start | bytes 24584 | tf_op jit(solution)/shard_map/ppermute | solution.py:557
  135.9 1.2 collective-permute-start.25
  137.1 3.7 %collective-permute-start.26 = (f32[8,256]{1,0:T(8,128)S(1)}, f32[8,256]{1,0:T(8,128)S(1)}, u32[]{:S(2)}, u32[]{:S(2)}) collective-permute-start(f32[8,256]{1,0:T(8,128)S(1)} %total.18.refs_0_), channel_id=1, source_target_pairs={{0,8},{4,12},{8,0},{12,4},{16,24},{20,28},{24,16},{28,20},{1,9},{5... | collective-permute-start | bytes 24584 | tf_op jit(solution)/shard_map/ppermute | solution.py:557
  137.7 4.6 %collective-permute-start.27 = (f32[8,256]{1,0:T(8,128)S(1)}, f32[8,256]{1,0:T(8,128)S(1)}, u32[]{:S(2)}, u32[]{:S(2)}) collective-permute-start(f32[8,256]{1,0:T(8,128)S(1)} %total.18.refs_0_), channel_id=1, source_target_pairs={{0,16},{4,20},{8,24},{12,28},{16,0},{20,4},{24,8},{28,12},{1,17},{... | collective-permute-start | bytes 24584 | tf_op jit(solution)/shard_map/ppermute | solution.py:557
  140.8 4.7 %collective-permute-start.28 = (f32[8,256]{1,0:T(8,128)S(1)}, f32[8,256]{1,0:T(8,128)S(1)}, u32[]{:S(2)}, u32[]{:S(2)}) collective-permute-start(f32[8,256]{1,0:T(8,128)S(1)} %total.18.refs_0_), channel_id=1, source_target_pairs={{0,24},{4,28},{8,16},{12,20},{16,8},{20,12},{24,0},{28,4},{1,25},{... | collective-permute-start | bytes 24584 | tf_op jit(solution)/shard_map/ppermute | solution.py:557
  142.3 23.2 %collective-permute-start.31 = (f32[512,256]{1,0:T(8,128)S(1)}, f32[512,256]{1,0:T(8,128)S(1)}, u32[]{:S(2)}, u32[]{:S(2)}) collective-permute-start(f32[512,256]{1,0:T(8,128)S(1)} %get-tuple-element.74), channel_id=1, source_target_pairs={{0,16},{4,20},{8,24},{12,28},{16,0},{20,4},{24,8},{28,12},{1,17},{... | collective-permute-start | bytes 1572872 | tf_op jit(solution)/shard_map/ppermute | solution.py:557
  145.4 20.5 %collective-permute-start.29 = (f32[512,256]{1,0:T(8,128)S(1)}, f32[512,256]{1,0:T(8,128)S(1)}, u32[]{:S(2)}, u32[]{:S(2)}) collective-permute-start(f32[512,256]{1,0:T(8,128)S(1)} %get-tuple-element.73), channel_id=1, source_target_pairs={{0,8},{4,12},{8,0},{12,4},{16,24},{20,28},{24,16},{28,20},{1,9},{5... | collective-permute-start | bytes 1572872 | tf_op jit(solution)/shard_map/ppermute | solution.py:557
  146.0 19.4 %collective-permute-start.18 = (f32[384,256]{1,0:T(8,128)S(1)}, f32[384,256]{1,0:T(8,128)S(1)}, u32[]{:S(2)}, u32[]{:S(2)}) collective-permute-start(f32[384,256]{1,0:T(8,128)S(1)} %get-tuple-element.67), channel_id=1, source_target_pairs={{0,8},{4,12},{8,0},{12,4},{16,24},{20,28},{24,16},{28,20},{1,9},{5... | collective-permute-start | bytes 1179656 | tf_op jit(solution)/shard_map/ppermute | solution.py:557
  165.4 21.5 %collective-permute-start.22 = (f32[384,256]{1,0:T(8,128)S(1)}, f32[384,256]{1,0:T(8,128)S(1)}, u32[]{:S(2)}, u32[]{:S(2)}) collective-permute-start(f32[384,256]{1,0:T(8,128)S(1)} %collective-permute-done.21.refs_2_), channel_id=1, source_target_pairs={{0,4},{4,0},{8,12},{12,8},{16,20},{20,16},{24,28},{28,24},{1,5},{5... | collective-permute-start | bytes 1179656 | tf_op jit(solution)/shard_map/ppermute | solution.py:557
  165.5 21.5 %collective-permute-start.19 = (f32[384,256]{1,0:T(8,128)S(1)}, f32[384,256]{1,0:T(8,128)S(1)}, u32[]{:S(2)}, u32[]{:S(2)}) collective-permute-start(f32[384,256]{1,0:T(8,128)S(1)} %collective-permute-done.18.refs_0_), channel_id=1, source_target_pairs={{0,4},{4,0},{8,12},{12,8},{16,20},{20,16},{24,28},{28,24},{1,5},{5... | collective-permute-start | bytes 1179656 | tf_op jit(solution)/shard_map/ppermute | solution.py:557
  166.0 13.4 %collective-permute-start.32 = (f32[512,256]{1,0:T(8,128)S(1)}, f32[512,256]{1,0:T(8,128)S(1)}, u32[]{:S(2)}, u32[]{:S(2)}) collective-permute-start(f32[512,256]{1,0:T(8,128)S(1)} %collective-permute-done.31.refs_2_), channel_id=1, source_target_pairs={{0,4},{4,0},{8,12},{12,8},{16,20},{20,16},{24,28},{28,24},{1,5},{5... | collective-permute-start | bytes 1572872 | tf_op jit(solution)/shard_map/ppermute | solution.py:557
  166.0 13.3 %collective-permute-start.30 = (f32[512,256]{1,0:T(8,128)S(1)}, f32[512,256]{1,0:T(8,128)S(1)}, u32[]{:S(2)}, u32[]{:S(2)}) collective-permute-start(f32[512,256]{1,0:T(8,128)S(1)} %collective-permute-done.29.refs_0_), channel_id=1, source_target_pairs={{0,4},{4,0},{8,12},{12,8},{16,20},{20,16},{24,28},{28,24},{1,5},{5... | collective-permute-start | bytes 1572872 | tf_op jit(solution)/shard_map/ppermute | solution.py:557
